TPU v7x, 8 devices: a whole 2x2x1 slice. The times are simulated.
8 devices in a mesh: g: 8 (over z, y, x, core).
Axes of the slice: x: 2, y: 2, z: 1, core: 2. Of those that a mesh axis runs over, the one named last changes fastest.
Arguments:
- node_feat: bfloat16 [4096, 1536], P(None, 'g')
- w_self1: bfloat16 [1536, 128], P('g')
- w_nbr1: bfloat16 [1536, 128], P('g')
- nbr_ids: int32 [4096, 10], P('g')
- nbr_mask: int32 [4096, 10], P('g')
- w_self2: bfloat16 [128, 128], replicated
- w_nbr2: bfloat16 [128, 128], replicated
- w_self3: bfloat16 [128, 7], replicated
- w_nbr3: bfloat16 [128, 7], replicated
Outputs:
- output: float32 [4096, 7], P('g')
All inputs are finite; a program needn't handle non-finite values.
Results may differ from a plain program's by a relative error of at most 0.00933618.
Values are sent between devices in bfloat16 or wider.
A program may use at most 1 GiB of HBM per device.

v0:
```python
import jax
import jax.numpy as jnp
from jax import lax
from jax.sharding import PartitionSpec as P, NamedSharding


def slot_total(row_data, nbr_ids, mask_f):
    def add_slot(acc_sum, slot_cols):
        ids_col, mask_col = slot_cols
        picked = jnp.take(row_data, ids_col, axis=0).astype(jnp.float32)
        return acc_sum + mask_col[:, None] * picked, None

    zero_acc = jnp.zeros((nbr_ids.shape[0], row_data.shape[1]), jnp.float32)
    slot_sum, _ = lax.scan(add_slot, zero_acc, (nbr_ids.T, mask_f.T))
    return slot_sum


def solution(mesh):
    def device_step(feat_cols, self_rows1, nbr_rows1, ids_local, mask_local, w_self2, w_nbr2, w_self3, w_nbr3):
        ids_all = lax.all_gather(ids_local, "g", tiled=True)
        mask_all = lax.all_gather(mask_local, "g", tiled=True).astype(jnp.float32)
        inv_all = 1.0 / jnp.sum(mask_all, axis=1, keepdims=True)
        self_part = jnp.dot(feat_cols, self_rows1, preferred_element_type=jnp.float32)
        nbr_proj = jnp.dot(feat_cols, nbr_rows1, preferred_element_type=jnp.float32)
        part_sum = self_part + slot_total(nbr_proj, ids_all, mask_all) * inv_all
        pre_one = lax.psum_scatter(part_sum, "g", scatter_dimension=0, tiled=True)
        hidden1 = jax.nn.relu(pre_one).astype(jnp.bfloat16)
        mask_bf = mask_local.astype(jnp.bfloat16)
        inv_local = 1.0 / jnp.sum(mask_local.astype(jnp.float32), axis=1, keepdims=True)

        def nbr_average(rows_local):
            rows_all = lax.all_gather(rows_local, "g", tiled=True)
            gathered = jnp.take(rows_all, ids_local, axis=0)
            summed = jnp.einsum("nk,nkh->nh", mask_bf, gathered, preferred_element_type=jnp.float32)
            return (summed * inv_local).astype(jnp.bfloat16)

        mean_one = nbr_average(hidden1)
        pre_two = jnp.dot(hidden1, w_self2, preferred_element_type=jnp.float32) + jnp.dot(mean_one, w_nbr2, preferred_element_type=jnp.float32)
        hidden2 = jax.nn.relu(pre_two).astype(jnp.bfloat16)
        mean_two = nbr_average(hidden2)
        return jnp.dot(hidden2, w_self3, preferred_element_type=jnp.float32) + jnp.dot(mean_two, w_nbr3, preferred_element_type=jnp.float32)

    col_split = P(None, "g")
    row_split = P("g", None)
    replicated = P()
    return jax.shard_map(
        device_step,
        mesh=mesh,
        in_specs=(col_split, row_split, row_split, row_split, row_split, replicated, replicated, replicated, replicated),
        out_specs=row_split,
        check_vma=False,
    )
```

profile of v0, /device:TPU:0, one launch (start us, length us, event | category | flops | bytes accessed | tf_op | source)
XLA Modules:
  0.0 363.7 jit_solution(3648365006448669799)
XLA Ops:
  6.5 14.5 %all_gather.12 = s32[4096,10]{0,1:T(8,128)S(1)} all-gather(s32[512,10]{0,1:T(8,128)} %param.17), channel_id=1, replica_groups=mesh['g'=8] {'g'}, dimensions={0}, use_global_device_ids=true | all-gather | bytes 184320 | tf_op jit(solution)/shard_map/all_gather | solution.py:21
  21.1 11.5 %all_gather.13 = s32[4096,10]{0,1:T(8,128)S(1)} all-gather(s32[512,10]{0,1:T(8,128)} %param.16), channel_id=1, replica_groups=mesh['g'=8] {'g'}, dimensions={0}, use_global_device_ids=true | all-gather | bytes 184320 | tf_op jit(solution)/shard_map/all_gather | solution.py:20
  35.5 205.9 %while.11 = (s32[]{:T(128)}, f32[4096,128]{1,0:T(8,128)}, f32[10,4096]{1,0:T(8,128)S(1)}, s32[10,4096]{1,0:T(8,128)S(1)}, f32[4096,128]{1,0:T(8,128)}, /*index=5*/s32[]{:T(128)}, s32[]{:T(128)}) while((s32[]{:T(128)}, f32[4096,128]{1,0:T(8,128)}, f32[10,4096]{1,0:T(8,128)S(1)}, s32[10,4096]{1,0:T(8,128)S(1)}, ...), condition=%wide.region_1.2_spmd.clone, body=%wide.region_0.0_spmd.clone.sunk | while | flops 2138115 | bytes 10657887 | solution.py:14
  35.6 15.8 %gather_fusion = f32[4096,128]{1,0:T(8,128)} fusion(f32[4096,128]{1,0:T(8,128)} %get-tuple-element.117, s32[4096]{0:T(1024)S(1)} %broadcast_clamp_fusion.3), kind=kCustom, calls=%fused_computation.clone.clone.1 | custom fusion | bytes 4210688 | tf_op jit(solution)/shard_map/while/body/eval_jaxpr/jit(_take)/gather | solution.py:10
  55.9 15.8 %gather_fusion = f32[4096,128]{1,0:T(8,128)} fusion(f32[4096,128]{1,0:T(8,128)} %get-tuple-element.117, s32[4096]{0:T(1024)S(1)} %broadcast_clamp_fusion.3), kind=kCustom, calls=%fused_computation.clone.clone.1 | custom fusion | bytes 4210688 | tf_op jit(solution)/shard_map/while/body/eval_jaxpr/jit(_take)/gather | solution.py:10
  71.7 4.8 %select_add_fusion.2 = f32[4096,128]{1,0:T(8,128)} fusion(f32[4096,128]{1,0:T(8,128)} %get-tuple-element.107, f32[4096,128]{1,0:T(8,128)} %gather_fusion, f32[4096]{0:T(1024)S(1)} %bitcast.34, pred[4096]{0:T(1024)(128)(4,1)S(1)} %compare_and_fusion.3, pred[]{:T(512)S(6)} %compare.3), kind=kLoop, calls=%fused_computation.3.clone.1 | loop fusion | flops 2097152 | bytes 6311937 | tf_op jit(solution)/shard_map/while/body/eval_jaxpr/add | solution.py:11
  76.5 15.8 %gather_fusion = f32[4096,128]{1,0:T(8,128)} fusion(f32[4096,128]{1,0:T(8,128)} %get-tuple-element.117, s32[4096]{0:T(1024)S(1)} %broadcast_clamp_fusion.3), kind=kCustom, calls=%fused_computation.clone.clone.1 | custom fusion | bytes 4210688 | tf_op jit(solution)/shard_map/while/body/eval_jaxpr/jit(_take)/gather | solution.py:10
  97.1 15.8 %gather_fusion = f32[4096,128]{1,0:T(8,128)} fusion(f32[4096,128]{1,0:T(8,128)} %get-tuple-element.117, s32[4096]{0:T(1024)S(1)} %broadcast_clamp_fusion.3), kind=kCustom, calls=%fused_computation.clone.clone.1 | custom fusion | bytes 4210688 | tf_op jit(solution)/shard_map/while/body/eval_jaxpr/jit(_take)/gather | solution.py:10
  112.9 4.8 %select_add_fusion.2 = f32[4096,128]{1,0:T(8,128)} fusion(f32[4096,128]{1,0:T(8,128)} %get-tuple-element.107, f32[4096,128]{1,0:T(8,128)} %gather_fusion, f32[4096]{0:T(1024)S(1)} %bitcast.34, pred[4096]{0:T(1024)(128)(4,1)S(1)} %compare_and_fusion.3, pred[]{:T(512)S(6)} %compare.3), kind=kLoop, calls=%fused_computation.3.clone.1 | loop fusion | flops 2097152 | bytes 6311937 | tf_op jit(solution)/shard_map/while/body/eval_jaxpr/add | solution.py:11
  117.7 15.8 %gather_fusion = f32[4096,128]{1,0:T(8,128)} fusion(f32[4096,128]{1,0:T(8,128)} %get-tuple-element.117, s32[4096]{0:T(1024)S(1)} %broadcast_clamp_fusion.3), kind=kCustom, calls=%fused_computation.clone.clone.1 | custom fusion | bytes 4210688 | tf_op jit(solution)/shard_map/while/body/eval_jaxpr/jit(_take)/gather | solution.py:10
  138.4 15.8 %gather_fusion = f32[4096,128]{1,0:T(8,128)} fusion(f32[4096,128]{1,0:T(8,128)} %get-tuple-element.117, s32[4096]{0:T(1024)S(1)} %broadcast_clamp_fusion.3), kind=kCustom, calls=%fused_computation.clone.clone.1 | custom fusion | bytes 4210688 | tf_op jit(solution)/shard_map/while/body/eval_jaxpr/jit(_take)/gather | solution.py:10
  154.2 4.8 %select_add_fusion.2 = f32[4096,128]{1,0:T(8,128)} fusion(f32[4096,128]{1,0:T(8,128)} %get-tuple-element.107, f32[4096,128]{1,0:T(8,128)} %gather_fusion, f32[4096]{0:T(1024)S(1)} %bitcast.34, pred[4096]{0:T(1024)(128)(4,1)S(1)} %compare_and_fusion.3, pred[]{:T(512)S(6)} %compare.3), kind=kLoop, calls=%fused_computation.3.clone.1 | loop fusion | flops 2097152 | bytes 6311937 | tf_op jit(solution)/shard_map/while/body/eval_jaxpr/add | solution.py:11
  159.0 15.8 %gather_fusion = f32[4096,128]{1,0:T(8,128)} fusion(f32[4096,128]{1,0:T(8,128)} %get-tuple-element.117, s32[4096]{0:T(1024)S(1)} %broadcast_clamp_fusion.3), kind=kCustom, calls=%fused_computation.clone.clone.1 | custom fusion | bytes 4210688 | tf_op jit(solution)/shard_map/while/body/eval_jaxpr/jit(_take)/gather | solution.py:10
  174.8 4.8 %select_add_fusion.2 = f32[4096,128]{1,0:T(8,128)} fusion(f32[4096,128]{1,0:T(8,128)} %get-tuple-element.107, f32[4096,128]{1,0:T(8,128)} %gather_fusion, f32[4096]{0:T(1024)S(1)} %bitcast.34, pred[4096]{0:T(1024)(128)(4,1)S(1)} %compare_and_fusion.3, pred[]{:T(512)S(6)} %compare.3), kind=kLoop, calls=%fused_computation.3.clone.1 | loop fusion | flops 2097152 | bytes 6311937 | tf_op jit(solution)/shard_map/while/body/eval_jaxpr/add | solution.py:11
  179.6 15.8 %gather_fusion = f32[4096,128]{1,0:T(8,128)} fusion(f32[4096,128]{1,0:T(8,128)} %get-tuple-element.117, s32[4096]{0:T(1024)S(1)} %broadcast_clamp_fusion.3), kind=kCustom, calls=%fused_computation.clone.clone.1 | custom fusion | bytes 4210688 | tf_op jit(solution)/shard_map/while/body/eval_jaxpr/jit(_take)/gather | solution.py:10
  195.4 4.8 %select_add_fusion.2 = f32[4096,128]{1,0:T(8,128)} fusion(f32[4096,128]{1,0:T(8,128)} %get-tuple-element.107, f32[4096,128]{1,0:T(8,128)} %gather_fusion, f32[4096]{0:T(1024)S(1)} %bitcast.34, pred[4096]{0:T(1024)(128)(4,1)S(1)} %compare_and_fusion.3, pred[]{:T(512)S(6)} %compare.3), kind=kLoop, calls=%fused_computation.3.clone.1 | loop fusion | flops 2097152 | bytes 6311937 | tf_op jit(solution)/shard_map/while/body/eval_jaxpr/add | solution.py:11
  200.2 15.8 %gather_fusion = f32[4096,128]{1,0:T(8,128)} fusion(f32[4096,128]{1,0:T(8,128)} %get-tuple-element.117, s32[4096]{0:T(1024)S(1)} %broadcast_clamp_fusion.3), kind=kCustom, calls=%fused_computation.clone.clone.1 | custom fusion | bytes 4210688 | tf_op jit(solution)/shard_map/while/body/eval_jaxpr/jit(_take)/gather | solution.py:10
  216.1 4.8 %select_add_fusion.2 = f32[4096,128]{1,0:T(8,128)} fusion(f32[4096,128]{1,0:T(8,128)} %get-tuple-element.107, f32[4096,128]{1,0:T(8,128)} %gather_fusion, f32[4096]{0:T(1024)S(1)} %bitcast.34, pred[4096]{0:T(1024)(128)(4,1)S(1)} %compare_and_fusion.3, pred[]{:T(512)S(6)} %compare.3), kind=kLoop, calls=%fused_computation.3.clone.1 | loop fusion | flops 2097152 | bytes 6311937 | tf_op jit(solution)/shard_map/while/body/eval_jaxpr/add | solution.py:11
  220.9 15.8 %gather_fusion = f32[4096,128]{1,0:T(8,128)} fusion(f32[4096,128]{1,0:T(8,128)} %get-tuple-element.117, s32[4096]{0:T(1024)S(1)} %broadcast_clamp_fusion.3), kind=kCustom, calls=%fused_computation.clone.clone.1 | custom fusion | bytes 4210688 | tf_op jit(solution)/shard_map/while/body/eval_jaxpr/jit(_take)/gather | solution.py:10
  245.1 32.7 %reduce-scatter.2.cloned.1.call-done = f32[512,128]{1,0:T(8,128)} async-done(((f32[4096,128]{1,0:T(8,128)}), f32[512,128]{1,0:T(8,128)}) %reduce-scatter.2.cloned.1.call-update) | async-done | bytes 262160 | tf_op jit(solution)/shard_map/reduce_scatter | solution.py:26
  281.4 15.8 %all-gather.3.cloned.1.call-done = bf16[4096,128]{1,0:T(8,128)(2,1)} async-done(((bf16[512,128]{1,0:T(8,128)(2,1)}), bf16[4096,128]{1,0:T(8,128)(2,1)}) %all-gather.3.cloned.1.call-update) | async-done | bytes 1048592 | tf_op jit(solution)/shard_map/all_gather | solution.py:32
  297.2 15.1 %gather_fusion.1 = bf16[5120,128]{1,0:T(8,128)(2,1)S(1)} fusion(bf16[4096,128]{1,0:T(8,128)(2,1)} %all-gather.3.cloned.1.call-done, s32[5120]{0:T(1024)S(1)} %broadcast_clamp_fusion.1), kind=kCustom, calls=%fused_computation.1.clone | custom fusion | bytes 2641920 | tf_op jit(solution)/shard_map/jit(_take)/gather | solution.py:33
  319.4 16.7 %all-gather.5.cloned.1.call-done = bf16[4096,128]{1,0:T(8,128)(2,1)} async-done(((bf16[512,128]{1,0:T(8,128)(2,1)}), bf16[4096,128]{1,0:T(8,128)(2,1)}) %all-gather.5.cloned.1.call-update) | async-done | bytes 1048592 | tf_op jit(solution)/shard_map/all_gather | solution.py:32
  336.0 15.1 %gather_fusion.2 = bf16[5120,128]{1,0:T(8,128)(2,1)S(1)} fusion(bf16[4096,128]{1,0:T(8,128)(2,1)} %all-gather.5.cloned.1.call-done, s32[5120]{0:T(1024)S(1)} %broadcast_clamp_fusion.1), kind=kCustom, calls=%fused_computation.2.clone | custom fusion | bytes 2641920 | tf_op jit(solution)/shard_map/jit(_take)/gather | solution.py:33
  (91 shorter events, 42.5 us)
Async XLA Ops:
  6.5 26.1 %copy-start = (bf16[4096,192]{0,1:T(8,128)(2,1)S(1)}, bf16[4096,192]{0,1:T(8,128)(2,1)}, u32[]{:S(2)}) copy-start(bf16[4096,192]{0,1:T(8,128)(2,1)} %param.13) | copy-start | bytes 4718596
  6.5 271.2 %reduce-scatter.2.cloned.1.call-start = ((), (), s32[]{:S(2)}) async-start(), calls=%async_computation.1 | async-start | bytes 2359296 | tf_op jit(solution)/shard_map/reduce_scatter | solution.py:26
  35.5 205.9 %copy-start.3 = (bf16[192,128]{1,0:T(8,128)(2,1)S(1)}, bf16[192,128]{1,0:T(8,128)(2,1)}, u32[]{:S(2)}) copy-start(bf16[192,128]{1,0:T(8,128)(2,1)} %param.14) | copy-start | bytes 147460
  245.0 34.4 %copy-start.1 = (s32[512,10]{0,1:T(8,128)S(1)}, s32[512,10]{0,1:T(8,128)}, u32[]{:S(2)}) copy-start(s32[512,10]{0,1:T(8,128)} %param.16) | copy-start | bytes 61444
  245.0 34.8 %copy-start.2 = (s32[512,10]{0,1:T(8,128)S(1)}, s32[512,10]{0,1:T(8,128)}, u32[]{:S(2)}) copy-start(s32[512,10]{0,1:T(8,128)} %param.17) | copy-start | bytes 61444
  245.0 35.3 %copy-start.4 = (bf16[128,128]{1,0:T(8,128)(2,1)S(1)}, bf16[128,128]{1,0:T(8,128)(2,1)}, u32[]{:S(2)}) copy-start(bf16[128,128]{1,0:T(8,128)(2,1)} %param.18) | copy-start | bytes 98308
  245.0 52.1 %all-gather.3.cloned.1.call-start = ((), (), s32[]{:S(2)}) async-start(), calls=%async_computation.2 | async-start | bytes 1179648 | tf_op jit(solution)/shard_map/all_gather | solution.py:32
  279.4 56.6 %all-gather.5.cloned.1.call-start = ((), (), s32[]{:S(2)}) async-start(), calls=%async_computation.3 | async-start | bytes 1179648 | tf_op jit(solution)/shard_map/all_gather | solution.py:32
  313.8 3.5 copy-start.5
  313.8 4.5 %copy-start.6 = (bf16[128,7]{0,1:T(8,128)(2,1)S(1)}, bf16[128,7]{0,1:T(8,128)(2,1)}, u32[]{:S(2)}) copy-start(bf16[128,7]{0,1:T(8,128)(2,1)} %param.20) | copy-start | bytes 5380
  352.7 3.6 copy-start.7
Sparse Core Ops, SparseCore 0:
  245.2 32.5 reduce-scatter.1
  279.6 17.5 all-gather.2
  318.5 17.5 all-gather.4
where the time goes:
time: 365 us; the launch traced here: 364 us
  local copies, waits for them, and re-layouts  192 us (53%)
  waiting for transfers between devices  65.2 us (18%)
  other arithmetic  49.5 us (14%)
  blocking collectives  26 us (7%)
  matrix products  17.4 us (5%)
  between operations  13.3 us (4%)
    gather x10, local copies, waits for them, and re-layouts, add_slot(): picked = jnp.take(row_data, ids_col, axis=0).astype(jnp.float32)  158 us
    add x10, other arithmetic, add_slot(): return (acc_sum + mask_col[:, None] * picked, None)  47.3 us
    gather x4, local copies, waits for them, and re-layouts, nbr_average(): gathered = jnp.take(rows_all, ids_local, axis=0)  33.3 us
    reduce_scatter x1, waiting for transfers between devices, device_step(): pre_one = lax.psum_scatter(part_sum, 'g', scatter_dimension=0, tiled=True)  32.7 us
    all_gather x2, waiting for transfers between devices, nbr_average(): rows_all = lax.all_gather(rows_local, 'g', tiled=True)  32.5 us
    all_gather x1, blocking collectives, device_step(): mask_all = lax.all_gather(mask_local, 'g', tiled=True).astype(jnp.float32)  14.5 us
    all_gather x1, blocking collectives, device_step(): ids_all = lax.all_gather(ids_local, 'g', tiled=True)  11.5 us
  transfers between devices with their start and end apart: 3, of which 3 were waited for; matrix products, arithmetic and copies ran while one was open for 1% of the time, Pallas kernels for 0%

commit v1 on v0

v1 whole, which is shorter than its diff:
```python
import jax
import jax.numpy as jnp
from jax import lax
from jax.experimental import pallas as pl
from jax.experimental.pallas import tpu as pltpu
from jax.sharding import PartitionSpec as P

MESH = pl.DeviceIdType.MESH
N_DEV = 8
NODES = 4096
BLK = NODES // N_DEV
HALF = NODES // 2
FAN = 10
HID = 128
TILE = 256
LANES = 256
GROUPS = BLK // LANES
BF = jnp.bfloat16
F32 = jnp.float32


def spread_ids(ids_s32, idb, wb, inv, slot):
    for g in range(GROUPS):
        cols = slice(g * LANES, (g + 1) * LANES)
        words, weights = [], []
        degree = jnp.zeros((8, LANES), F32)
        for k in range(FAN):
            raw = jnp.broadcast_to(ids_s32[slot, k : k + 1, cols], (8, LANES))
            valid = raw >= 0
            degree += jnp.where(valid, 1.0, 0.0)
            upper = raw >= HALF
            word = jnp.where(upper, raw - HALF, raw)
            weight = jnp.where(valid, jnp.where(upper, 1.0, 0.0625), 0.0)
            for m in range(k):
                same = word == words[m]
                weights[m] = weights[m] + jnp.where(same, weight, 0.0)
                word = jnp.where(same, -1, word)
            words.append(word)
            weights.append(weight)
        inv[slot, :, cols] = 1.0 / degree
        for k in range(FAN):
            idb[slot, g, k] = words[k].astype(jnp.int16)
            wb[slot, g, k] = weights[k].astype(BF)


def build_tile(first_row, row_ids, idb, wb, slot, store_low, store_high):
    start = row_ids[...] + jnp.full((8, LANES), first_row, jnp.int32).astype(jnp.int16)
    for g in range(GROUPS):
        ids = [idb[slot, g, k] for k in range(FAN)]
        wts = [wb[slot, g, k] for k in range(FAN)]
        rows = start
        for r in range(TILE // 8):
            acc = jnp.zeros((8, LANES), BF)
            for k in range(FAN):
                acc = jnp.where(ids[k] == rows, wts[k], acc)
            high = jnp.floor(acc)
            store_high(r * 8, g * LANES, high)
            store_low(r * 8, g * LANES, (acc - high) * jnp.array(16.0, BF))
            rows = rows + jnp.array(8, jnp.int16)


def kernel(
    x_hbm, ws1, wn1, ids_in, mask_in, ws2, wn2, ws3t, wn3t, out_ref,
    x_v, w1t, w2st, w2nt, yown, yrecv, ysum, sown, ssend, srecv,
    ids_pkt, ids_rcv, ids_s32, row_ids, idb, wb, inv,
    lo0, hi0, lo1, hi1, a_own, acc, zacc, rs_send, rs_recv, h1, h2,
    x_sem, ids_ss, ids_rs, y_ss, y_rs, s_ss, s_rs, r_ss, r_rs, g1_ss, g1_rs, g2_ss, g2_rs,
):
    me = lax.axis_index("g")
    core = lax.rem(me, 2)
    cx = lax.rem(me // 2, 2)
    cy = me // 4
    partner = me + 1 - 2 * core
    peer_x = me + 2 - 4 * cx
    peer_y = me + 4 - 8 * cy
    peer_d = me + 6 - 4 * cx - 8 * cy
    peers = (peer_d, peer_y, peer_x)

    barrier = pltpu.get_barrier_semaphore()
    for peer in (peer_d, peer_y, peer_x, partner):
        pl.semaphore_signal(barrier, inc=1, device_id=(peer,), device_id_type=MESH)

    x_copies = []
    for b in range(N_DEV):
        cp = pltpu.make_async_copy(x_hbm.at[:, pl.ds(b * BLK, BLK)], x_v.at[b], x_sem.at[b])
        cp.start()
        x_copies.append(cp)

    def remote(src, dst, ss, rs, dev):
        return pltpu.make_async_remote_copy(
            src_ref=src, dst_ref=dst, send_sem=ss, recv_sem=rs, device_id=(dev,), device_id_type=MESH
        )

    masked = jnp.where(mask_in[...] > 0, ids_in[...], -1)
    ids_pkt[...] = jnp.full(ids_pkt.shape, -1, jnp.int16)
    ids_pkt[0:FAN, :] = masked.astype(jnp.int16)
    ids_s32[3, 0:FAN, :] = masked
    w1t[0:HID, :] = ws1[...].T
    w1t[HID:, :] = wn1[...].T
    w2st[...] = ws2[...].T
    w2nt[...] = wn2[...].T
    acc[...] = jnp.zeros_like(acc)

    pl.semaphore_wait(barrier, 4)
    sends = []
    id_copies = [remote(ids_pkt, ids_rcv.at[s], ids_ss.at[s], ids_rs.at[s], peers[s]) for s in range(3)]
    for cp in id_copies:
        cp.start()
    sends += id_copies

    for cp in x_copies:
        cp.wait()
    y_copies, s_copies = [], []
    for i in range(4):
        b = 2 * i + 1 - core
        part = jnp.dot(w1t[...], x_v[b], preferred_element_type=F32)
        yown[b] = part[HID:].astype(BF)
        ssend[i] = part[:HID].astype(BF)
        y_copies.append(remote(yown.at[b], yrecv.at[b], y_ss.at[2 * i], y_rs.at[2 * i + 1], partner))
        s_copies.append(remote(ssend.at[i], srecv.at[i], s_ss.at[i], s_rs.at[i], partner))
        b2 = 2 * i + core
        part2 = jnp.dot(w1t[...], x_v[b2], preferred_element_type=F32)
        yown[b2] = part2[HID:].astype(BF)
        sown[i] = part2[:HID]
        y_copies.append(remote(yown.at[b2], yrecv.at[b2], y_ss.at[2 * i + 1], y_rs.at[2 * i], partner))
        y_copies[-2].start()
        s_copies[-1].start()
        y_copies[-1].start()
    sends += y_copies + s_copies

    row_ids[...] = lax.broadcasted_iota(jnp.int32, (8, LANES), 0).astype(jnp.int16)
    spread_ids(ids_s32, idb, wb, inv, 3)

    def own_step(c, carry):
        for par in range(2):

            def put(half):
                def store(r, l, v):
                    a_own[half * 4 + c, par * TILE + r : par * TILE + r + 8, l : l + LANES] = v

                return store

            build_tile(c * 2 * TILE + par * TILE, row_ids, idb, wb, 3, put(0), put(1))
        return carry

    lax.fori_loop(0, 4, own_step, 0)

    for s in range(3):
        id_copies[s].wait_recv()
        ids_s32[s] = ids_rcv[s].astype(jnp.int32)
        spread_ids(ids_s32, idb, wb, inv, s)
    for cp in y_copies:
        cp.wait_recv()
    for cp in s_copies:
        cp.wait_recv()
    for b in range(N_DEV):
        ysum[b] = yown[b] + yrecv[b]

    bufs = ((lo0, hi0), (lo1, hi1))

    def put_into(ref):
        def store(r, l, v):
            ref[r : r + 8, l : l + LANES] = v

        return store

    def build_into(par, flat, slot):
        lo, hi = bufs[par]
        build_tile(lax.rem(flat, 8) * TILE, row_ids, idb, wb, slot, put_into(lo), put_into(hi))

    def dot_from(par, cc):
        lo, hi = bufs[par]
        cols = slice(par * TILE, (par + 1) * TILE)
        return jnp.dot(ysum[cc, :, cols], lo[...], preferred_element_type=F32) + jnp.dot(
            ysum[4 + cc, :, cols], hi[...], preferred_element_type=F32
        )

    def rs_copy(s):
        return remote(rs_send.at[s], rs_recv.at[s], r_ss.at[s], r_rs.at[s], peers[s])

    build_into(0, 0, 0)

    def rs_step(p, carry):
        s = p // 4
        cc = lax.rem(p, 4)
        acc[...] += dot_from(0, cc)
        build_into(1, 2 * p + 1, s)
        acc[...] += dot_from(1, cc)
        build_into(0, 2 * p + 2, lax.rem((2 * p + 2) // 8, 3))
        for t in range(3):

            @pl.when(p == 4 * t + 3)
            def _():
                chip = peers[t] // 2
                total = acc[...] * jnp.broadcast_to(inv[t, 0:1, :], (HID, BLK)) + sown[chip] + srecv[chip].astype(F32)
                rs_send[t] = total.astype(BF)
                acc[...] = jnp.zeros_like(acc)
                rs_copy(t).start()

        return carry

    lax.fori_loop(0, 12, rs_step, 0)
    rs_copies = [rs_copy(t) for t in range(3)]
    sends += rs_copies

    def own_dot(h, b):
        return jnp.dot(h[b], a_own[b], preferred_element_type=F32)

    inv_own = jnp.broadcast_to(inv[3, 0:1, :], (HID, BLK))
    zacc[...] = own_dot(ysum, 0)
    for b in range(1, N_DEV):
        zacc[...] += own_dot(ysum, b)
    chip_me = me // 2
    zacc[...] = zacc[...] * inv_own + sown[chip_me] + srecv[chip_me].astype(F32)
    for t in range(3):
        rs_copies[t].wait_recv()
        zacc[...] += rs_recv[t].astype(F32)
    h1[me] = jnp.maximum(zacc[...], 0.0).astype(BF)

    def gather_mean(h, ss, rs):
        first = [remote(h.at[me], h.at[me], ss.at[t], rs.at[t], peers[t]) for t in range(3)]
        to_partner = remote(h.at[me], h.at[me], ss.at[3], rs.at[3], partner)
        for cp in first:
            cp.start()
        to_partner.start()
        acc[...] = own_dot(h, me)
        to_partner.wait_recv()
        acc[...] += own_dot(h, partner)
        forwards = []
        for t in (1, 2, 0):
            first[t].wait_recv()
            fwd = remote(h.at[peers[t]], h.at[peers[t]], ss.at[4 + t], rs.at[4 + t], partner)
            fwd.start()
            forwards.append((t, fwd))
        for t in (1, 2, 0):
            acc[...] += own_dot(h, peers[t])
        for t, fwd in forwards:
            fwd.wait_recv()
            acc[...] += own_dot(h, peers[t] + 1 - 2 * core)
        return first + [to_partner] + [f for _, f in forwards]

    sends += gather_mean(h1, g1_ss, g1_rs)
    mean1 = (acc[...] * jnp.broadcast_to(inv[3, 0:1, :], (HID, BLK))).astype(BF)
    pre2 = jnp.dot(w2st[...], h1[me], preferred_element_type=F32) + jnp.dot(
        w2nt[...], mean1, preferred_element_type=F32
    )
    h2[me] = jnp.maximum(pre2, 0.0).astype(BF)
    sends += gather_mean(h2, g2_ss, g2_rs)
    mean2 = (acc[...] * jnp.broadcast_to(inv[3, 0:1, :], (HID, BLK))).astype(BF)
    out_ref[...] = jnp.dot(ws3t[...], h2[me], preferred_element_type=F32) + jnp.dot(
        wn3t[...], mean2, preferred_element_type=F32
    )
    for cp in sends:
        cp.wait_send()


def solution(mesh):
    def device_step(feat, ws1, wn1, ids, mask, ws2, wn2, ws3, wn3):
        vm = pl.BlockSpec(memory_space=pltpu.VMEM)
        dma = pltpu.SemaphoreType.DMA
        out_t = pl.pallas_call(
            kernel,
            out_shape=jax.ShapeDtypeStruct((7, BLK), F32),
            in_specs=[pl.BlockSpec(memory_space=pl.ANY)] + [vm] * 8,
            out_specs=vm,
            scratch_shapes=[
                pltpu.VMEM((N_DEV, 192, BLK), BF),
                pltpu.VMEM((2 * HID, 192), BF),
                pltpu.VMEM((HID, HID), BF),
                pltpu.VMEM((HID, HID), BF),
                pltpu.VMEM((N_DEV, HID, BLK), BF),
                pltpu.VMEM((N_DEV, HID, BLK), BF),
                pltpu.VMEM((N_DEV, HID, BLK), BF),
                pltpu.VMEM((4, HID, BLK), F32),
                pltpu.VMEM((4, HID, BLK), BF),
                pltpu.VMEM((4, HID, BLK), BF),
                pltpu.VMEM((16, BLK), jnp.int16),
                pltpu.VMEM((3, 16, BLK), jnp.int16),
                pltpu.VMEM((4, 16, BLK), jnp.int32),
                pltpu.VMEM((8, LANES), jnp.int16),
                pltpu.VMEM((4, GROUPS, FAN, 8, LANES), jnp.int16),
                pltpu.VMEM((4, GROUPS, FAN, 8, LANES), BF),
                pltpu.VMEM((4, 8, BLK), F32),
                pltpu.VMEM((TILE, BLK), BF),
                pltpu.VMEM((TILE, BLK), BF),
                pltpu.VMEM((TILE, BLK), BF),
                pltpu.VMEM((TILE, BLK), BF),
                pltpu.VMEM((N_DEV, BLK, BLK), BF),
                pltpu.VMEM((HID, BLK), F32),
                pltpu.VMEM((HID, BLK), F32),
                pltpu.VMEM((3, HID, BLK), BF),
                pltpu.VMEM((3, HID, BLK), BF),
                pltpu.VMEM((N_DEV, HID, BLK), BF),
                pltpu.VMEM((N_DEV, HID, BLK), BF),
                dma((N_DEV,)),
                dma((3,)), dma((3,)),
                dma((8,)), dma((8,)),
                dma((4,)), dma((4,)),
                dma((3,)), dma((3,)),
                dma((7,)), dma((7,)),
                dma((7,)), dma((7,)),
            ],
            compiler_params=pltpu.CompilerParams(
                collective_id=0, has_side_effects=True, vmem_limit_bytes=60 * 1024 * 1024
            ),
            name="graphsage",
        )(feat.T, ws1, wn1, ids.T, mask.T, ws2, wn2, ws3.T, wn3.T)
        return out_t.T

    col_split = P(None, "g")
    row_split = P("g", None)
    replicated = P()
    return jax.shard_map(
        device_step,
        mesh=mesh,
        in_specs=(col_split, row_split, row_split, row_split, row_split, replicated, replicated, replicated, replicated),
        out_specs=row_split,
        check_vma=False,
    )
```

time: 365 us -> 42 us (0.12)
  local copies, waits for them, and re-layouts: 192 us -> 1.32 us
  waiting for transfers between devices: 65.2 us -> 0 us
  other arithmetic: 49.5 us -> 0 us
  Pallas kernels: 0 us -> 40.5 us
  blocking collectives: 26 us -> 0 us
  matrix products: 17.4 us -> 0 us
  between operations: 13.3 us -> 0.01 us
    gather x14 -> x0, local copies, waits for them, and re-layouts: 191 us -> none  [the longest x10 158 us: add_slot(): picked = jnp.take(row_data, ids_col, axis=0).astype(jnp.float32)]
    add x10 -> x0, other arithmetic: 47.3 us -> none  [add_slot(): return (acc_sum + mask_col[:, None] * picked, None)]
    pallas_call x0 -> x1, Pallas kernels: none -> 40.5 us  [device_step(): pl.pallas_call(kernel, out_shape=jax.ShapeDtypeStruct((7, BLK), F32), in_...]
    reduce_scatter x1 -> x0, waiting for transfers between devices: 32.7 us -> none  [device_step(): pre_one = lax.psum_scatter(part_sum, 'g', scatter_dimension=0, tiled=True)]
    all_gather x2 -> x0, waiting for transfers between devices: 32.5 us -> none  [nbr_average(): rows_all = lax.all_gather(rows_local, 'g', tiled=True)]
    all_gather x2 -> x0, blocking collectives: 26 us -> none  [the longest x1 14.5 us: device_step(): mask_all = lax.all_gather(mask_local, 'g', tiled=True).astype(jnp.float32)]
    dot_general x8 -> x0, matrix products: 17.4 us -> none  [the longest x2 7.08 us: nbr_average(): jnp.einsum('nk,nkh->nh', mask_bf, gathered, preferred_element_type=jnp.fl...]
  transfers between devices with their start and end apart: 3 -> 0, of which waited for: 3 -> 0; matrix products, arithmetic and copies ran while one was open for 1% -> 0% of each run, Pallas kernels for 0% -> 0%
where the time goes in v1:
time: 42 us; the launch traced here: 41.8 us
  Pallas kernels  40.5 us (96%)
  local copies, waits for them, and re-layouts  1.32 us (3%)
    pallas_call x1, Pallas kernels, device_step(): pl.pallas_call(kernel, out_shape=jax.ShapeDtypeStruct((7, BLK), F32), in_...  40.5 us
    unnamed x1, local copies, waits for them, and re-layouts  1.32 us

profile of v1, /device:TPU:0, one launch (start us, length us, event | category | flops | bytes accessed | tf_op | source)
XLA Modules:
  0.0 41.8 jit_solution(42632589413689825)
XLA Ops:
  0.0 40.5 %graphsage.1 = f32[7,512]{1,0:T(8,128)} custom-call(bf16[192,4096]{1,0:T(8,128)(2,1)} %bitcast.6, bf16[192,128]{1,0:T(8,128)(2,1)} %ws1.1, bf16[192,128]{1,0:T(8,128)(2,1)} %wn1.1, s32[10,512]{1,0:T(8,128)} %bitcast.8, s32[10,512]{1,0:T(8,128)} %bitcast.9, bf16[128,128]{1,0:T(8,128)(2,1)} %ws2.1, bf16[128,128]{1,0:T(8,128)(2,1)} %wn2.1, ...), custom_call_target="tpu_custom_call" | custom-call | tf_op jit(solution)/shard_map/graphsage/pallas_call | solution.py:261
  40.5 1.3 %copy.11 = f32[512,7]{0,1:T(8,128)} copy(f32[512,7]{0,1:T(8,128)} %bitcast.7) | data formatting | bytes 28672

commit v2 on v1

v2 whole, which is shorter than its diff:
```python
import jax
import jax.numpy as jnp
from jax import lax
from jax.experimental import pallas as pl
from jax.experimental.pallas import tpu as pltpu
from jax.sharding import PartitionSpec as P

MESH = pl.DeviceIdType.MESH
N_DEV = 8
NODES = 4096
BLK = NODES // N_DEV
HALF = NODES // 2
FAN = 10
HID = 128
TILE = 256
LANES = 256
GROUPS = BLK // LANES
BF = jnp.bfloat16
F32 = jnp.float32


def spread_ids(ids_s32, idb, wb, inv, slot):
    for g in range(GROUPS):
        cols = slice(g * LANES, (g + 1) * LANES)
        words, weights = [], []
        degree = jnp.zeros((8, LANES), F32)
        for k in range(FAN):
            raw = jnp.broadcast_to(ids_s32[slot, k : k + 1, cols], (8, LANES))
            valid = raw >= 0
            degree += jnp.where(valid, 1.0, 0.0)
            upper = raw >= HALF
            word = jnp.where(upper, raw - HALF, raw)
            weight = jnp.where(valid, jnp.where(upper, 1.0, 0.0625), 0.0)
            for m in range(k):
                same = word == words[m]
                weights[m] = weights[m] + jnp.where(same, weight, 0.0)
                word = jnp.where(same, -1, word)
            words.append(word)
            weights.append(weight)
        inv[slot, :, cols] = 1.0 / degree
        for k in range(FAN):
            idb[slot, g, k] = words[k].astype(jnp.int16)
            wb[slot, g, k] = weights[k].astype(BF)


def build_tile(tile, row_ids, idb, wb, slot, groups, store_low, store_high):
    for g in groups:
        ids = [idb[slot, g, k] for k in range(FAN)]
        wts = [wb[slot, g, k] for k in range(FAN)]
        for r in range(TILE // 8):
            rows = row_ids[tile, r]
            acc = jnp.zeros((8, LANES), BF)
            for k in range(FAN):
                acc = jnp.where(ids[k] == rows, wts[k], acc)
            high = jnp.floor(acc)
            store_high(r * 8, g * LANES, high)
            store_low(r * 8, g * LANES, acc - high)


def kernel(
    x_hbm, ws1_hbm, wn1_hbm, ids_hbm, mask_hbm, ws2_hbm, wn2_hbm, ws3_hbm, wn3_hbm, out_ref,
    x_v, ws1, wn1, ids_in, mask_in, ws2, wn2, ws3t, wn3t,
    w1t, w2st, w2nt, yown, yrecv, ysum, sown, ssend, srecv,
    ids_pkt, ids_rcv, ids_s32, row_ids, idb, wb, inv,
    lo0, hi0, lo1, hi1, lo2, hi2, lo3, hi3, a_own, acc, rs_send, rs_recv, h1, h2,
    in_sem, x_sem, ids_ss, ids_rs, y_ss, y_rs, s_ss, s_rs, r_ss, r_rs, g1_ss, g1_rs, g2_ss, g2_rs,
):
    me = lax.axis_index("g")
    core = lax.rem(me, 2)
    cx = lax.rem(me // 2, 2)
    cy = me // 4
    partner = me + 1 - 2 * core
    peer_x = me + 2 - 4 * cx
    peer_y = me + 4 - 8 * cy
    peer_d = me + 6 - 4 * cx - 8 * cy
    peers = (peer_d, peer_y, peer_x)

    barrier = pltpu.get_barrier_semaphore()
    for peer in (peer_d, peer_y, peer_x, partner):
        pl.semaphore_signal(barrier, inc=1, device_id=(peer,), device_id_type=MESH)

    def fetch(src, dst, i):
        cp = pltpu.make_async_copy(src, dst, in_sem.at[i])
        cp.start()
        return cp

    ids_cp = fetch(ids_hbm, ids_in, 0)
    mask_cp = fetch(mask_hbm, mask_in, 1)
    w1_cps = [fetch(ws1_hbm, ws1, 2), fetch(wn1_hbm, wn1, 3)]
    x_copies = []
    for b in range(N_DEV):
        cp = pltpu.make_async_copy(x_hbm.at[:, pl.ds(b * BLK, BLK)], x_v.at[b], x_sem.at[b])
        cp.start()
        x_copies.append(cp)
    late_cps = [fetch(ws2_hbm, ws2, 4), fetch(wn2_hbm, wn2, 5), fetch(ws3_hbm, ws3t, 6), fetch(wn3_hbm, wn3t, 7)]

    def remote(src, dst, ss, rs, dev):
        return pltpu.make_async_remote_copy(
            src_ref=src, dst_ref=dst, send_sem=ss, recv_sem=rs, device_id=(dev,), device_id_type=MESH
        )

    for tile in range(HALF // TILE):
        for r in range(TILE // 8):
            rows = lax.broadcasted_iota(jnp.int32, (8, LANES), 0) + (tile * TILE + r * 8)
            row_ids[tile, r] = rows.astype(jnp.int16)
    ids_pkt[...] = jnp.full(ids_pkt.shape, -1, jnp.int16)
    ids_cp.wait()
    mask_cp.wait()
    masked = jnp.where(mask_in[...] > 0, ids_in[...], -1)
    ids_pkt[0:FAN, :] = masked.astype(jnp.int16)
    ids_s32[3, 0:FAN, :] = masked
    for cp in w1_cps:
        cp.wait()
    w1t[0:HID, :] = ws1[...].T
    w1t[HID:, :] = wn1[...].T

    pl.semaphore_wait(barrier, 4)
    sends = []
    id_copies = [remote(ids_pkt, ids_rcv.at[s], ids_ss.at[s], ids_rs.at[s], peers[s]) for s in range(3)]
    for cp in id_copies:
        cp.start()
    sends += id_copies

    for cp in x_copies:
        cp.wait()
    y_copies, s_copies = [], []
    for i in range(4):
        b = 2 * i + 1 - core
        part = jnp.dot(w1t[...], x_v[b], preferred_element_type=F32)
        yown[b] = part[HID:].astype(BF)
        ssend[i] = part[:HID].astype(BF)
        y_copies.append(remote(yown.at[b], yrecv.at[b], y_ss.at[2 * i], y_rs.at[2 * i + 1], partner))
        s_copies.append(remote(ssend.at[i], srecv.at[i], s_ss.at[i], s_rs.at[i], partner))
        b2 = 2 * i + core
        part2 = jnp.dot(w1t[...], x_v[b2], preferred_element_type=F32)
        yown[b2] = part2[HID:].astype(BF)
        sown[i] = part2[:HID]
        y_copies.append(remote(yown.at[b2], yrecv.at[b2], y_ss.at[2 * i + 1], y_rs.at[2 * i], partner))
        y_copies[-2].start()
        s_copies[-1].start()
        y_copies[-1].start()
    sends += y_copies + s_copies

    spread_ids(ids_s32, idb, wb, inv, 3)

    def own_step(c, carry):
        for par in range(2):

            def put(half):
                def store(r, l, v):
                    v = v if half else v * jnp.array(16.0, BF)
                    a_own[half * 4 + c, par * TILE + r : par * TILE + r + 8, l : l + LANES] = v

                return store

            build_tile(2 * c + par, row_ids, idb, wb, 3, range(GROUPS), put(0), put(1))
        return carry

    lax.fori_loop(0, 4, own_step, 0)
    for cp in late_cps:
        cp.wait()
    w2st[...] = ws2[...].T
    w2nt[...] = wn2[...].T

    ring = ((lo0, hi0), (lo1, hi1), (lo2, hi2), (lo3, hi3))

    def build_into(tile, slot, g):
        lo, hi = ring[tile % 4]

        def put_into(ref):
            def store(r, l, v):
                ref[r : r + 8, :] = v

            return store

        build_tile(tile, row_ids, idb, wb, slot, (g,), put_into(lo), put_into(hi))

    def dot_from(tile):
        lo, hi = ring[tile % 4]
        cols = slice(tile % 2 * TILE, (tile % 2 + 1) * TILE)
        low = jnp.dot(ysum[tile // 2, :, cols], lo[...], preferred_element_type=F32)
        high = jnp.dot(ysum[4 + tile // 2, :, cols], hi[...], preferred_element_type=F32)
        return low, high

    def lanes(g):
        return slice(g * LANES, (g + 1) * LANES)

    def take_ids(s):
        id_copies[s].wait_recv()
        ids_s32[s] = ids_rcv[s].astype(jnp.int32)
        spread_ids(ids_s32, idb, wb, inv, s)

    def unit(u):
        return lax.rem(1 + 2 * lax.rem(u, 3), 3), lax.rem(u // 3, 2)

    def rs_copy(s, g, peer):
        return remote(rs_send.at[s, g], rs_recv.at[s, g], r_ss.at[2 * s + g], r_rs.at[2 * s + g], peer)

    take_ids(1)
    build_into(0, 1, 0)
    for cp in y_copies:
        cp.wait_recv()
    for cp in s_copies:
        cp.wait_recv()
    for b in range(N_DEV):
        ysum[b] = yown[b] + yrecv[b]

    def unit_step(u, carry):
        s, g = unit(u)
        after_s, after_g = unit(u + 1)

        @pl.when(u == 0)
        def _():
            take_ids(0)

        @pl.when(u == 1)
        def _():
            take_ids(2)

        low = high = None
        for tile in range(8):
            part = dot_from(tile)
            if tile < 7:
                build_into(tile + 1, s, g)
            else:
                build_into(0, after_s, after_g)
            low = part[0] if low is None else low + part[0]
            high = part[1] if high is None else high + part[1]
        peer = me + (1 - lax.rem(s, 2)) * (2 - 4 * cx) + (1 - s // 2) * (4 - 8 * cy)
        cols = pl.ds(pl.multiple_of(g * LANES, LANES), LANES)
        chip = peer // 2
        total = (low * 16.0 + high) * jnp.broadcast_to(inv[s, 0:1, cols], (HID, LANES))
        total = total + sown[chip, :, cols] + srecv[chip, :, cols].astype(F32)
        rs_send[s, g] = total.astype(BF)
        rs_copy(s, g, peer).start()
        return carry

    lax.fori_loop(0, 6, unit_step, 0)
    rs_copies = {(s, g): rs_copy(s, g, peers[s]) for s in range(3) for g in range(2)}
    sends += list(rs_copies.values())

    chip_me = me // 2
    inv_own = jnp.broadcast_to(inv[3, 0:1, :], (HID, BLK))

    def own_dot(h, b, p):
        return jnp.dot(h[b, p], a_own[b, p * TILE : (p + 1) * TILE, :], preferred_element_type=F32)

    def gather_start(h, ss, rs, p):
        outs = [remote(h.at[me, p], h.at[me, p], ss.at[7 * p + t], rs.at[7 * p + t], peers[t]) for t in range(3)]
        outs.append(remote(h.at[me, p], h.at[me, p], ss.at[7 * p + 3], rs.at[7 * p + 3], partner))
        for cp in outs:
            cp.start()
        return outs

    def gather_finish(h, ss, rs, started):
        acc[...] = own_dot(h, me, 0) + own_dot(h, me, 1)
        for p in range(2):
            started[p][3].wait_recv()
            acc[...] += own_dot(h, partner, p)
        forwards = []
        for p in range(2):
            for t in (1, 2, 0):
                started[p][t].wait_recv()
                fwd = remote(
                    h.at[peers[t], p], h.at[peers[t], p], ss.at[7 * p + 4 + t], rs.at[7 * p + 4 + t], partner
                )
                fwd.start()
                forwards.append((t, p, fwd))
            for t in (1, 2, 0):
                acc[...] += own_dot(h, peers[t], p)
        for t, p, fwd in forwards:
            fwd.wait_recv()
            acc[...] += own_dot(h, peers[t] + 1 - 2 * core, p)
        return started[0] + started[1] + [f for _, _, f in forwards]

    started1 = []
    for g in range(2):
        own = jnp.dot(ysum[0], a_own[0, :, lanes(g)], preferred_element_type=F32)
        for b in range(1, N_DEV):
            own = own + jnp.dot(ysum[b], a_own[b, :, lanes(g)], preferred_element_type=F32)
        z = own * inv_own[:, lanes(g)] + sown[chip_me, :, lanes(g)] + srecv[chip_me, :, lanes(g)].astype(F32)
        for t in (1, 0, 2):
            rs_copies[t, g].wait_recv()
            z = z + rs_recv[t, g].astype(F32)
        h1[me, g] = jnp.maximum(z, 0.0).astype(BF)
        started1.append(gather_start(h1, g1_ss, g1_rs, g))
    sends += gather_finish(h1, g1_ss, g1_rs, started1)

    started2 = []
    for g in range(2):
        mean1 = (acc[:, lanes(g)] * inv_own[:, lanes(g)]).astype(BF)
        pre2 = jnp.dot(w2st[...], h1[me, g], preferred_element_type=F32) + jnp.dot(
            w2nt[...], mean1, preferred_element_type=F32
        )
        h2[me, g] = jnp.maximum(pre2, 0.0).astype(BF)
        started2.append(gather_start(h2, g2_ss, g2_rs, g))
    sends += gather_finish(h2, g2_ss, g2_rs, started2)
    for g in range(2):
        mean2 = (acc[:, lanes(g)] * inv_own[:, lanes(g)]).astype(BF)
        out_ref[:, lanes(g)] = jnp.dot(ws3t[...], h2[me, g], preferred_element_type=F32) + jnp.dot(
            wn3t[...], mean2, preferred_element_type=F32
        )
    for cp in sends:
        cp.wait_send()


def solution(mesh):
    def device_step(feat, ws1, wn1, ids, mask, ws2, wn2, ws3, wn3):
        vm = pl.BlockSpec(memory_space=pltpu.VMEM)
        dma = pltpu.SemaphoreType.DMA
        out_t = pl.pallas_call(
            kernel,
            out_shape=jax.ShapeDtypeStruct((7, BLK), F32),
            in_specs=[pl.BlockSpec(memory_space=pl.ANY)] * 9,
            out_specs=vm,
            scratch_shapes=[
                pltpu.VMEM((N_DEV, 192, BLK), BF),
                pltpu.VMEM((192, HID), BF),
                pltpu.VMEM((192, HID), BF),
                pltpu.VMEM((FAN, BLK), jnp.int32),
                pltpu.VMEM((FAN, BLK), jnp.int32),
                pltpu.VMEM((HID, HID), BF),
                pltpu.VMEM((HID, HID), BF),
                pltpu.VMEM((7, HID), BF),
                pltpu.VMEM((7, HID), BF),
                pltpu.VMEM((2 * HID, 192), BF),
                pltpu.VMEM((HID, HID), BF),
                pltpu.VMEM((HID, HID), BF),
                pltpu.VMEM((N_DEV, HID, BLK), BF),
                pltpu.VMEM((N_DEV, HID, BLK), BF),
                pltpu.VMEM((N_DEV, HID, BLK), BF),
                pltpu.VMEM((4, HID, BLK), F32),
                pltpu.VMEM((4, HID, BLK), BF),
                pltpu.VMEM((4, HID, BLK), BF),
                pltpu.VMEM((16, BLK), jnp.int16),
                pltpu.VMEM((3, 16, BLK), jnp.int16),
                pltpu.VMEM((4, 16, BLK), jnp.int32),
                pltpu.VMEM((HALF // TILE, TILE // 8, 8, LANES), jnp.int16),
                pltpu.VMEM((4, GROUPS, FAN, 8, LANES), jnp.int16),
                pltpu.VMEM((4, GROUPS, FAN, 8, LANES), BF),
                pltpu.VMEM((4, 8, BLK), F32),
                pltpu.VMEM((TILE, LANES), BF),
                pltpu.VMEM((TILE, LANES), BF),
                pltpu.VMEM((TILE, LANES), BF),
                pltpu.VMEM((TILE, LANES), BF),
                pltpu.VMEM((TILE, LANES), BF),
                pltpu.VMEM((TILE, LANES), BF),
                pltpu.VMEM((TILE, LANES), BF),
                pltpu.VMEM((TILE, LANES), BF),
                pltpu.VMEM((N_DEV, BLK, BLK), BF),
                pltpu.VMEM((HID, BLK), F32),
                pltpu.VMEM((3, 2, HID, LANES), BF),
                pltpu.VMEM((3, 2, HID, LANES), BF),
                pltpu.VMEM((N_DEV, 2, HID, LANES), BF),
                pltpu.VMEM((N_DEV, 2, HID, LANES), BF),
                dma((8,)),
                dma((N_DEV,)),
                dma((3,)), dma((3,)),
                dma((8,)), dma((8,)),
                dma((4,)), dma((4,)),
                dma((6,)), dma((6,)),
                dma((14,)), dma((14,)),
                dma((14,)), dma((14,)),
            ],
            compiler_params=pltpu.CompilerParams(
                collective_id=0, has_side_effects=True, vmem_limit_bytes=60 * 1024 * 1024
            ),
            name="graphsage",
        )(feat.T, ws1, wn1, ids.T, mask.T, ws2, wn2, ws3.T, wn3.T)
        return out_t.T

    col_split = P(None, "g")
    row_split = P("g", None)
    replicated = P()
    return jax.shard_map(
        device_step,
        mesh=mesh,
        in_specs=(col_split, row_split, row_split, row_split, row_split, replicated, replicated, replicated, replicated),
        out_specs=row_split,
        check_vma=False,
    )
```

time: 42 us -> 38.2 us (0.910)
  Pallas kernels: 40.5 us -> 36.7 us
    pallas_call x1, Pallas kernels: 40.5 us -> 36.7 us  [device_step(): pl.pallas_call(kernel, out_shape=jax.ShapeDtypeStruct((7, BLK), F32), in_...]
where the time goes in v2:
time: 38.2 us; the launch traced here: 38.1 us
  Pallas kernels  36.7 us (96%)
  local copies, waits for them, and re-layouts  1.32 us (3%)
    pallas_call x1, Pallas kernels, device_step(): pl.pallas_call(kernel, out_shape=jax.ShapeDtypeStruct((7, BLK), F32), in_...  36.7 us
    unnamed x1, local copies, waits for them, and re-layouts  1.32 us

profile of v2, /device:TPU:0, one launch (start us, length us, event | category | flops | bytes accessed | tf_op | source)
XLA Modules:
  0.0 38.1 jit_solution(10198980366817649235)
XLA Ops:
  0.0 36.7 %graphsage.1 = f32[7,512]{1,0:T(8,128)} custom-call(bf16[192,4096]{1,0:T(8,128)(2,1)} %bitcast.6, bf16[192,128]{1,0:T(8,128)(2,1)} %ws1_hbm.1, bf16[192,128]{1,0:T(8,128)(2,1)} %wn1_hbm.1, s32[10,512]{1,0:T(8,128)} %bitcast.8, s32[10,512]{1,0:T(8,128)} %bitcast.9, bf16[128,128]{1,0:T(8,128)(2,1)} %ws2_hbm.1, bf16[128,128]{1,0:T(8,128)(2,1)} %wn2_hbm.1, ...), custom_call_target="tpu_custom_call" | custom-call | tf_op jit(solution)/shard_map/graphsage/pallas_call | solution.py:311
  36.7 1.3 %copy.11 = f32[512,7]{0,1:T(8,128)} copy(f32[512,7]{0,1:T(8,128)} %bitcast.7) | data formatting | bytes 28672

commit v3 on v2

v3 whole, which is shorter than its diff:
```python
import jax
import jax.numpy as jnp
from jax import lax
from jax.experimental import pallas as pl
from jax.experimental.pallas import tpu as pltpu
from jax.sharding import PartitionSpec as P

MESH = pl.DeviceIdType.MESH
N_DEV = 8
NODES = 4096
BLK = NODES // N_DEV
HALF = NODES // 2
FAN = 10
HID = 128
TILE = 256
LANES = 256
BF = jnp.bfloat16
F32 = jnp.float32


UNITS = (((2, 0), (1, 0)), ((0, 0), (0, 1)), ((2, 1), (1, 1)), ((0, 2), (0, 3)), ((2, 2), (1, 2)), ((2, 3), (1, 3)))
OWN = 6
RING = 6
Q = 128


def spread_ids(ids_s32, idb, wb, inv, u):
    words, weights = [], []
    degree = jnp.zeros((8, LANES), F32)
    for k in range(FAN):
        raw = jnp.broadcast_to(ids_s32[u, k : k + 1, :], (8, LANES))
        valid = raw >= 0
        degree += jnp.where(valid, 1.0, 0.0)
        upper = raw >= HALF
        word = jnp.where(upper, raw - HALF, raw)
        weight = jnp.where(valid, jnp.where(upper, 1.0, 0.0625), 0.0)
        for m in range(k):
            same = word == words[m]
            weights[m] = weights[m] + jnp.where(same, weight, 0.0)
            word = jnp.where(same, -1, word)
        words.append(word)
        weights.append(weight)
    inv[u] = 1.0 / degree
    for k in range(FAN):
        idb[u, k] = words[k].astype(jnp.int16)
        wb[u, k] = weights[k].astype(BF)


def build_tile(tile, row_ids, idb, wb, u, store_low, store_high):
    ids = [idb[u, k] for k in range(FAN)]
    wts = [wb[u, k] for k in range(FAN)]
    for r in range(0, TILE // 8, 8):
        rows = row_ids[tile, r : r + 8]
        acc = jnp.zeros((8, 8, LANES), BF)
        for k in range(FAN):
            acc = jnp.where(ids[k][None] == rows, wts[k][None], acc)
        high = jnp.floor(acc)
        store_high(r, high)
        store_low(r, acc - high)


def kernel(
    x_hbm, ws1_hbm, wn1_hbm, ids_hbm, mask_hbm, ws2_hbm, wn2_hbm, ws3_hbm, wn3_hbm, out_ref,
    x_v, ws1, wn1, ids_in, mask_in, ws2, wn2, ws3t, wn3t,
    w1t, w2st, w2nt, yown, yrecv, ysum, sown, ssend, srecv,
    ids_pkt, ids_rcv, ids_s32, row_ids, idb, wb, inv,
    ring, a_own, acc, zbase, rs_send, rs_recv, h1, h2,
    in_sem, x_sem, ids_ss, ids_rs, y_ss, y_rs, s_ss, s_rs, r_ss, r_rs, g1_ss, g1_rs, g2_ss, g2_rs,
):
    me = lax.axis_index("g")
    core = lax.rem(me, 2)
    cx = lax.rem(me // 2, 2)
    cy = me // 4
    partner = me + 1 - 2 * core
    peer_x = me + 2 - 4 * cx
    peer_y = me + 4 - 8 * cy
    peer_d = me + 6 - 4 * cx - 8 * cy
    peers = (peer_d, peer_y, peer_x)

    barrier = pltpu.get_barrier_semaphore()
    for peer in (peer_d, peer_y, peer_x, partner):
        pl.semaphore_signal(barrier, inc=1, device_id=(peer,), device_id_type=MESH)

    def fetch(src, dst, i):
        cp = pltpu.make_async_copy(src, dst, in_sem.at[i])
        cp.start()
        return cp

    ids_cp = fetch(ids_hbm, ids_in, 0)
    mask_cp = fetch(mask_hbm, mask_in, 1)
    w1_cps = [fetch(ws1_hbm, ws1, 2), fetch(wn1_hbm, wn1, 3)]
    x_copies = []
    for b in range(N_DEV):
        cp = pltpu.make_async_copy(x_hbm.at[:, pl.ds(b * BLK, BLK)], x_v.at[b], x_sem.at[b])
        cp.start()
        x_copies.append(cp)
    late_cps = [fetch(ws2_hbm, ws2, 4), fetch(wn2_hbm, wn2, 5), fetch(ws3_hbm, ws3t, 6), fetch(wn3_hbm, wn3t, 7)]

    def remote(src, dst, ss, rs, dev):
        return pltpu.make_async_remote_copy(
            src_ref=src, dst_ref=dst, send_sem=ss, recv_sem=rs, device_id=(dev,), device_id_type=MESH
        )

    row_shape = (TILE // 8, 8, LANES)
    row_base = lax.broadcasted_iota(jnp.int32, row_shape, 0) * 8 + lax.broadcasted_iota(jnp.int32, row_shape, 1)
    for tile in range(HALF // TILE):
        row_ids[tile] = (row_base + tile * TILE).astype(jnp.int16)
    ids_pkt[...] = jnp.full(ids_pkt.shape, -1, jnp.int16)
    ids_cp.wait()
    mask_cp.wait()
    masked = jnp.where(mask_in[...] > 0, ids_in[...], -1)
    ids_pkt[0:FAN, :] = masked.astype(jnp.int16)
    for g in range(2):
        ids_s32[OWN + g, 0:FAN, :] = masked[:, g * LANES : (g + 1) * LANES]
        spread_ids(ids_s32, idb, wb, inv, OWN + g)
    for cp in w1_cps:
        cp.wait()
    w1t[0:HID, :] = ws1[...].T
    w1t[HID:, :] = wn1[...].T

    pl.semaphore_wait(barrier, 4)
    sends = []
    id_copies = [remote(ids_pkt, ids_rcv.at[s], ids_ss.at[s], ids_rs.at[s], peers[s]) for s in range(3)]
    for cp in id_copies:
        cp.start()
    sends += id_copies

    def build_own(tile):
        def put(half, g):
            def store(r, v):
                v = v if half else v * jnp.array(16.0, BF)
                row = tile % 2 * (TILE // 8) + r
                a_own[half * 4 + tile // 2, row : row + 8, :, g * LANES : (g + 1) * LANES] = v

            return store

        for g in range(2):
            build_tile(tile, row_ids, idb, wb, OWN + g, put(0, g), put(1, g))

    for cp in x_copies:
        cp.wait()
    y_copies, s_copies = [], []
    for i in range(4):
        b = 2 * i + 1 - core
        part = jnp.dot(w1t[...], x_v[b], preferred_element_type=F32)
        yown[b] = part[HID:].astype(BF)
        ssend[i] = part[:HID].astype(BF)
        build_own(2 * i)
        y_copies.append(remote(yown.at[b], yrecv.at[b], y_ss.at[2 * i], y_rs.at[2 * i + 1], partner))
        s_copies.append(remote(ssend.at[i], srecv.at[i], s_ss.at[i], s_rs.at[i], partner))
        b2 = 2 * i + core
        part2 = jnp.dot(w1t[...], x_v[b2], preferred_element_type=F32)
        yown[b2] = part2[HID:].astype(BF)
        sown[i] = part2[:HID]
        y_copies.append(remote(yown.at[b2], yrecv.at[b2], y_ss.at[2 * i + 1], y_rs.at[2 * i], partner))
        y_copies[-2].start()
        y_copies[-1].start()
        build_own(2 * i + 1)
    for cp in s_copies:
        cp.start()
    sends += y_copies + s_copies
    for cp in late_cps:
        cp.wait()
    w2st[...] = ws2[...].T
    w2nt[...] = wn2[...].T

    def build_into(flat):
        def put(half):
            def store(r, v):
                ring[flat % RING, half, r : r + 8] = v

            return store

        build_tile(flat % 8, row_ids, idb, wb, flat // 8, put(0), put(1))

    def dot_from(flat):
        tile = flat % 8
        cols = slice(tile % 2 * TILE, (tile % 2 + 1) * TILE)
        low = ring[flat % RING, 0].reshape(TILE, LANES)
        high = ring[flat % RING, 1].reshape(TILE, LANES)
        return (
            jnp.dot(ysum[tile // 2, :, cols], low, preferred_element_type=F32),
            jnp.dot(ysum[4 + tile // 2, :, cols], high, preferred_element_type=F32),
        )

    def lanes(g):
        return slice(g * LANES, (g + 1) * LANES)

    def quarter(q):
        return slice(q * Q, (q + 1) * Q)

    def take_ids(s):
        id_copies[s].wait_recv()
        for u, pair in enumerate(UNITS):
            for half, (slot, q) in enumerate(pair):
                if slot == s:
                    ids_s32[u, :, quarter(half)] = ids_rcv[s, :, quarter(q)].astype(jnp.int32)

    chip_me = me // 2
    rs_copies = {}
    started1 = []

    def finish_unit(u, low, high):
        total = (low * 16.0 + high) * jnp.broadcast_to(inv[u, 0:1, :], (HID, LANES))
        for half, (s, q) in enumerate(UNITS[u]):
            chip = peers[s] // 2
            part = total[:, quarter(half)] + sown[chip, :, quarter(q)] + srecv[chip, :, quarter(q)].astype(F32)
            rs_send[s, q] = part.astype(BF)
            rs_copies[s, q] = remote(rs_send.at[s, q], rs_recv.at[s, q], r_ss.at[4 * s + q], r_rs.at[4 * s + q], peers[s])
            rs_copies[s, q].start()

    def gather_start(h, ss, rs, p):
        outs = [remote(h.at[me, p], h.at[me, p], ss.at[7 * p + t], rs.at[7 * p + t], peers[t]) for t in range(3)]
        outs.append(remote(h.at[me, p], h.at[me, p], ss.at[7 * p + 3], rs.at[7 * p + 3], partner))
        for cp in outs:
            cp.start()
        return outs

    def finish_quarter(q):
        z = zbase[q // 2, :, quarter(q % 2)]
        for t in (1, 2, 0):
            rs_copies[t, q].wait_recv()
            z = z + rs_recv[t, q].astype(F32)
        h1[me, q] = jnp.maximum(z, 0.0).astype(BF)
        started1.append(gather_start(h1, g1_ss, g1_rs, q))

    def own_base(g, own):
        base = own * jnp.broadcast_to(inv[OWN + g, 0:1, :], (HID, LANES))
        zbase[g] = base + sown[chip_me, :, lanes(g)] + srecv[chip_me, :, lanes(g)].astype(F32)

    take_ids(2)
    take_ids(1)
    spread_ids(ids_s32, idb, wb, inv, 0)
    lead = 3
    for flat in range(lead):
        build_into(flat)
    for cp in y_copies:
        cp.wait_recv()
    for b in range(N_DEV):
        ysum[b] = yown[b] + yrecv[b]
    take_ids(0)
    built = lead
    low = high = own = None
    for flat in range(48):
        u, tile = flat // 8, flat % 8
        while built < 48 and built - flat < 2 or (built < 48 and tile % 2 == 0 and built - flat < lead):
            if built % 8 == 0:
                spread_ids(ids_s32, idb, wb, inv, built // 8)
            build_into(built)
            built += 1
        part = dot_from(flat)
        low = part[0] if low is None else low + part[0]
        high = part[1] if high is None else high + part[1]
        if u in (1, 3):
            piece = jnp.dot(ysum[tile], a_own[tile, :, :, lanes(u // 2)].reshape(BLK, LANES), preferred_element_type=F32)
            own = piece if own is None else own + piece
        if tile == 7:
            if u == 0:
                for cp in s_copies:
                    cp.wait_recv()
            finish_unit(u, low, high)
            low = high = None
            if u in (1, 3):
                own_base(u // 2, own)
                own = None
            if u == 4:
                finish_quarter(0)
    finish_quarter(1)
    finish_quarter(2)
    finish_quarter(3)
    sends += list(rs_copies.values())

    inv_own = jnp.concatenate(
        [jnp.broadcast_to(inv[OWN + g, 0:1, :], (HID, LANES)) for g in range(2)], axis=1
    )

    def own_dot(h, b, p, size):
        rows = a_own[b, p * size // 8 : (p + 1) * size // 8].reshape(size, BLK)
        return jnp.dot(h[b, p], rows, preferred_element_type=F32)

    def gather_finish(h, ss, rs, started, size):
        pieces = BLK // size
        acc[...] = sum(own_dot(h, me, p, size) for p in range(pieces))
        forwards = []

        def take_forwards(p):
            for fwd in forwards[p]:
                fwd.wait_recv()
            acc[...] += sum(own_dot(h, peers[t] + 1 - 2 * core, p, size) for t in range(3))

        for p in range(pieces):
            group = []
            for t in (1, 2, 0):
                started[p][t].wait_recv()
                fwd = remote(
                    h.at[peers[t], p], h.at[peers[t], p], ss.at[7 * p + 4 + t], rs.at[7 * p + 4 + t], partner
                )
                fwd.start()
                group.append(fwd)
            forwards.append(group)
            started[p][3].wait_recv()
            acc[...] += sum(own_dot(h, dev, p, size) for dev in (*peers, partner))
            if p > 0:
                take_forwards(p - 1)
        take_forwards(pieces - 1)
        return [cp for outs in started for cp in outs] + [cp for group in forwards for cp in group]

    sends += gather_finish(h1, g1_ss, g1_rs, started1, Q)

    started2 = []
    for g in range(2):
        mean1 = (acc[:, lanes(g)] * inv_own[:, lanes(g)]).astype(BF)
        mine = jnp.concatenate([h1[me, 2 * g], h1[me, 2 * g + 1]], axis=1)
        pre2 = jnp.dot(w2st[...], mine, preferred_element_type=F32) + jnp.dot(
            w2nt[...], mean1, preferred_element_type=F32
        )
        h2[me, g] = jnp.maximum(pre2, 0.0).astype(BF)
        started2.append(gather_start(h2, g2_ss, g2_rs, g))
    for g in range(2):
        out_ref[:, lanes(g)] = jnp.dot(ws3t[...], h2[me, g], preferred_element_type=F32)
    sends += gather_finish(h2, g2_ss, g2_rs, started2, LANES)
    for g in range(2):
        mean2 = (acc[:, lanes(g)] * inv_own[:, lanes(g)]).astype(BF)
        out_ref[:, lanes(g)] += jnp.dot(wn3t[...], mean2, preferred_element_type=F32)
    for cp in sends:
        cp.wait_send()


def solution(mesh):
    def device_step(feat, ws1, wn1, ids, mask, ws2, wn2, ws3, wn3):
        vm = pl.BlockSpec(memory_space=pltpu.VMEM)
        dma = pltpu.SemaphoreType.DMA
        out_t = pl.pallas_call(
            kernel,
            out_shape=jax.ShapeDtypeStruct((7, BLK), F32),
            in_specs=[pl.BlockSpec(memory_space=pl.ANY)] * 9,
            out_specs=vm,
            scratch_shapes=[
                pltpu.VMEM((N_DEV, 192, BLK), BF),
                pltpu.VMEM((192, HID), BF),
                pltpu.VMEM((192, HID), BF),
                pltpu.VMEM((FAN, BLK), jnp.int32),
                pltpu.VMEM((FAN, BLK), jnp.int32),
                pltpu.VMEM((HID, HID), BF),
                pltpu.VMEM((HID, HID), BF),
                pltpu.VMEM((7, HID), BF),
                pltpu.VMEM((7, HID), BF),
                pltpu.VMEM((2 * HID, 192), BF),
                pltpu.VMEM((HID, HID), BF),
                pltpu.VMEM((HID, HID), BF),
                pltpu.VMEM((N_DEV, HID, BLK), BF),
                pltpu.VMEM((N_DEV, HID, BLK), BF),
                pltpu.VMEM((N_DEV, HID, BLK), BF),
                pltpu.VMEM((4, HID, BLK), F32),
                pltpu.VMEM((4, HID, BLK), BF),
                pltpu.VMEM((4, HID, BLK), BF),
                pltpu.VMEM((16, BLK), jnp.int16),
                pltpu.VMEM((3, 16, BLK), jnp.int16),
                pltpu.VMEM((8, 16, LANES), jnp.int32),
                pltpu.VMEM((HALF // TILE, TILE // 8, 8, LANES), jnp.int16),
                pltpu.VMEM((8, FAN, 8, LANES), jnp.int16),
                pltpu.VMEM((8, FAN, 8, LANES), BF),
                pltpu.VMEM((8, 8, LANES), F32),
                pltpu.VMEM((RING, 2, TILE // 8, 8, LANES), BF),
                pltpu.VMEM((N_DEV, BLK // 8, 8, BLK), BF),
                pltpu.VMEM((HID, BLK), F32),
                pltpu.VMEM((2, HID, LANES), F32),
                pltpu.VMEM((3, 4, HID, Q), BF),
                pltpu.VMEM((3, 4, HID, Q), BF),
                pltpu.VMEM((N_DEV, 4, HID, Q), BF),
                pltpu.VMEM((N_DEV, 2, HID, LANES), BF),
                dma((8,)),
                dma((N_DEV,)),
                dma((3,)), dma((3,)),
                dma((8,)), dma((8,)),
                dma((4,)), dma((4,)),
                dma((12,)), dma((12,)),
                dma((28,)), dma((28,)),
                dma((14,)), dma((14,)),
            ],
            compiler_params=pltpu.CompilerParams(
                collective_id=0, has_side_effects=True, vmem_limit_bytes=60 * 1024 * 1024
            ),
            name="graphsage",
        )(feat.T, ws1, wn1, ids.T, mask.T, ws2, wn2, ws3.T, wn3.T)
        return out_t.T

    col_split = P(None, "g")
    row_split = P("g", None)
    replicated = P()
    return jax.shard_map(
        device_step,
        mesh=mesh,
        in_specs=(col_split, row_split, row_split, row_split, row_split, replicated, replicated, replicated, replicated),
        out_specs=row_split,
        check_vma=False,
    )
```

time: 38.2 us -> 37.1 us (0.971)
  Pallas kernels: 36.7 us -> 35.5 us
    pallas_call x1, Pallas kernels: 36.7 us -> 35.5 us  [device_step(): pl.pallas_call(kernel, out_shape=jax.ShapeDtypeStruct((7, BLK), F32), in_...]
where the time goes in v3:
time: 37.1 us; the launch traced here: 36.9 us
  Pallas kernels  35.5 us (96%)
  local copies, waits for them, and re-layouts  1.32 us (4%)
    pallas_call x1, Pallas kernels, device_step(): pl.pallas_call(kernel, out_shape=jax.ShapeDtypeStruct((7, BLK), F32), in_...  35.5 us
    unnamed x1, local copies, waits for them, and re-layouts  1.32 us

profile of v3, /device:TPU:0, one launch (start us, length us, event | category | flops | bytes accessed | tf_op | source)
XLA Modules:
  0.0 36.9 jit_solution(6870323630794588329)
XLA Ops:
  0.0 35.5 %graphsage.1 = f32[7,512]{1,0:T(8,128)} custom-call(bf16[192,4096]{1,0:T(8,128)(2,1)} %bitcast.6, bf16[192,128]{1,0:T(8,128)(2,1)} %ws1_hbm.1, bf16[192,128]{1,0:T(8,128)(2,1)} %wn1_hbm.1, s32[10,512]{1,0:T(8,128)} %bitcast.8, s32[10,512]{1,0:T(8,128)} %bitcast.9, bf16[128,128]{1,0:T(8,128)(2,1)} %ws2_hbm.1, bf16[128,128]{1,0:T(8,128)(2,1)} %wn2_hbm.1, ...), custom_call_target="tpu_custom_call" | custom-call | tf_op jit(solution)/shard_map/graphsage/pallas_call | solution.py:333
  35.5 1.3 %copy.11 = f32[512,7]{0,1:T(8,128)} copy(f32[512,7]{0,1:T(8,128)} %bitcast.7) | data formatting | bytes 28672

commit v4 on v3

--- a/solution.py
+++ b/solution.py
@@ -18,8 +18,9 @@
 F32 = jnp.float32
 
 
-UNITS = (((2, 0), (1, 0)), ((0, 0), (0, 1)), ((2, 1), (1, 1)), ((0, 2), (0, 3)), ((2, 2), (1, 2)), ((2, 3), (1, 3)))
+UNITS = (((0, 0), (0, 1)), ((2, 0), (1, 0)), ((2, 1), (1, 1)), ((0, 2), (0, 3)), ((2, 2), (1, 2)), ((2, 3), (1, 3)))
 OWN = 6
+OWN_EARLY = 3
 RING = 6
 Q = 128
 
@@ -72,13 +73,13 @@
     cx = lax.rem(me // 2, 2)
     cy = me // 4
     partner = me + 1 - 2 * core
-    peer_x = me + 2 - 4 * cx
-    peer_y = me + 4 - 8 * cy
-    peer_d = me + 6 - 4 * cx - 8 * cy
-    peers = (peer_d, peer_y, peer_x)
+    steps = (6 - 4 * cx - 8 * cy, 4 - 8 * cy, 2 - 4 * cx)
+    peers = tuple(partner + step for step in steps)
+    mates = tuple(me + step for step in steps)
+    mine, theirs = (me, *peers), (partner, *mates)
 
     barrier = pltpu.get_barrier_semaphore()
-    for peer in (peer_d, peer_y, peer_x, partner):
+    for peer in (*peers, partner):
         pl.semaphore_signal(barrier, inc=1, device_id=(peer,), device_id_type=MESH)
 
     def fetch(src, dst, i):
@@ -141,24 +142,23 @@
         cp.wait()
     y_copies, s_copies = [], []
     for i in range(4):
-        b = 2 * i + 1 - core
-        part = jnp.dot(w1t[...], x_v[b], preferred_element_type=F32)
-        yown[b] = part[HID:].astype(BF)
+        part = jnp.dot(w1t[...], x_v[theirs[i]], preferred_element_type=F32)
+        yown[theirs[i]] = part[HID:].astype(BF)
         ssend[i] = part[:HID].astype(BF)
-        build_own(2 * i)
-        y_copies.append(remote(yown.at[b], yrecv.at[b], y_ss.at[2 * i], y_rs.at[2 * i + 1], partner))
+        part2 = jnp.dot(w1t[...], x_v[mine[i]], preferred_element_type=F32)
+        yown[mine[i]] = part2[HID:].astype(BF)
+        sown[i] = part2[:HID]
+        for j, b in enumerate((theirs[i], mine[i])):
+            y_copies.append(remote(yown.at[b], yrecv.at[b], y_ss.at[2 * i + j], y_rs.at[2 * i + j], partner))
+            y_copies[-1].start()
         s_copies.append(remote(ssend.at[i], srecv.at[i], s_ss.at[i], s_rs.at[i], partner))
-        b2 = 2 * i + core
-        part2 = jnp.dot(w1t[...], x_v[b2], preferred_element_type=F32)
-        yown[b2] = part2[HID:].astype(BF)
-        sown[i] = part2[:HID]
-        y_copies.append(remote(yown.at[b2], yrecv.at[b2], y_ss.at[2 * i + 1], y_rs.at[2 * i], partner))
-        y_copies[-2].start()
-        y_copies[-1].start()
-        build_own(2 * i + 1)
+        if i < OWN_EARLY:
+            build_own(i)
     for cp in s_copies:
         cp.start()
     sends += y_copies + s_copies
+    for tile in range(OWN_EARLY, 8):
+        build_own(tile)
     for cp in late_cps:
         cp.wait()
     w2st[...] = ws2[...].T
@@ -196,15 +196,13 @@
                 if slot == s:
                     ids_s32[u, :, quarter(half)] = ids_rcv[s, :, quarter(q)].astype(jnp.int32)
 
-    chip_me = me // 2
     rs_copies = {}
     started1 = []
 
     def finish_unit(u, low, high):
         total = (low * 16.0 + high) * jnp.broadcast_to(inv[u, 0:1, :], (HID, LANES))
         for half, (s, q) in enumerate(UNITS[u]):
-            chip = peers[s] // 2
-            part = total[:, quarter(half)] + sown[chip, :, quarter(q)] + srecv[chip, :, quarter(q)].astype(F32)
+            part = total[:, quarter(half)] + sown[1 + s, :, quarter(q)] + srecv[1 + s, :, quarter(q)].astype(F32)
             rs_send[s, q] = part.astype(BF)
             rs_copies[s, q] = remote(rs_send.at[s, q], rs_recv.at[s, q], r_ss.at[4 * s + q], r_rs.at[4 * s + q], peers[s])
             rs_copies[s, q].start()
@@ -226,10 +224,9 @@
 
     def own_base(g, own):
         base = own * jnp.broadcast_to(inv[OWN + g, 0:1, :], (HID, LANES))
-        zbase[g] = base + sown[chip_me, :, lanes(g)] + srecv[chip_me, :, lanes(g)].astype(F32)
-
-    take_ids(2)
-    take_ids(1)
+        zbase[g] = base + sown[0, :, lanes(g)] + srecv[0, :, lanes(g)].astype(F32)
+
+    take_ids(0)
     spread_ids(ids_s32, idb, wb, inv, 0)
     lead = 3
     for flat in range(lead):
@@ -238,7 +235,8 @@
         cp.wait_recv()
     for b in range(N_DEV):
         ysum[b] = yown[b] + yrecv[b]
-    take_ids(0)
+    take_ids(2)
+    take_ids(1)
     built = lead
     low = high = own = None
     for flat in range(48):
@@ -278,15 +276,17 @@
         rows = a_own[b, p * size // 8 : (p + 1) * size // 8].reshape(size, BLK)
         return jnp.dot(h[b, p], rows, preferred_element_type=F32)
 
-    def gather_finish(h, ss, rs, started, size):
+    def gather_finish(h, ss, rs, started, size, old_sends):
         pieces = BLK // size
         acc[...] = sum(own_dot(h, me, p, size) for p in range(pieces))
+        for cp in old_sends:
+            cp.wait_send()
         forwards = []
 
         def take_forwards(p):
             for fwd in forwards[p]:
                 fwd.wait_recv()
-            acc[...] += sum(own_dot(h, peers[t] + 1 - 2 * core, p, size) for t in range(3))
+            acc[...] += sum(own_dot(h, mate, p, size) for mate in mates)
 
         for p in range(pieces):
             group = []
@@ -305,7 +305,7 @@
         take_forwards(pieces - 1)
         return [cp for outs in started for cp in outs] + [cp for group in forwards for cp in group]
 
-    sends += gather_finish(h1, g1_ss, g1_rs, started1, Q)
+    sends = gather_finish(h1, g1_ss, g1_rs, started1, Q, sends)
 
     started2 = []
     for g in range(2):
@@ -318,7 +318,7 @@
         started2.append(gather_start(h2, g2_ss, g2_rs, g))
     for g in range(2):
         out_ref[:, lanes(g)] = jnp.dot(ws3t[...], h2[me, g], preferred_element_type=F32)
-    sends += gather_finish(h2, g2_ss, g2_rs, started2, LANES)
+    sends = gather_finish(h2, g2_ss, g2_rs, started2, LANES, sends)
     for g in range(2):
         mean2 = (acc[:, lanes(g)] * inv_own[:, lanes(g)]).astype(BF)
         out_ref[:, lanes(g)] += jnp.dot(wn3t[...], mean2, preferred_element_type=F32)

time: 37.1 us -> 36.6 us (0.987)
  Pallas kernels: 35.5 us -> 35.1 us
    pallas_call x1, Pallas kernels: 35.5 us -> 35.1 us  [device_step(): pl.pallas_call(kernel, out_shape=jax.ShapeDtypeStruct((7, BLK), F32), in_...]
where the time goes in v4:
time: 36.6 us; the launch traced here: 36.4 us
  Pallas kernels  35.1 us (96%)
  local copies, waits for them, and re-layouts  1.32 us (4%)
    pallas_call x1, Pallas kernels, device_step(): pl.pallas_call(kernel, out_shape=jax.ShapeDtypeStruct((7, BLK), F32), in_...  35.1 us
    unnamed x1, local copies, waits for them, and re-layouts  1.32 us

profile of v4, /device:TPU:0, one launch (start us, length us, event | category | flops | bytes accessed | tf_op | source)
XLA Modules:
  0.0 36.4 jit_solution(2693911906862420423)
XLA Ops:
  0.0 35.1 %graphsage.1 = f32[7,512]{1,0:T(8,128)} custom-call(bf16[192,4096]{1,0:T(8,128)(2,1)} %bitcast.6, bf16[192,128]{1,0:T(8,128)(2,1)} %ws1_hbm.1, bf16[192,128]{1,0:T(8,128)(2,1)} %wn1_hbm.1, s32[10,512]{1,0:T(8,128)} %bitcast.8, s32[10,512]{1,0:T(8,128)} %bitcast.9, bf16[128,128]{1,0:T(8,128)(2,1)} %ws2_hbm.1, bf16[128,128]{1,0:T(8,128)(2,1)} %wn2_hbm.1, ...), custom_call_target="tpu_custom_call" | custom-call | tf_op jit(solution)/shard_map/graphsage/pallas_call | solution.py:333
  35.1 1.3 %copy.11 = f32[512,7]{0,1:T(8,128)} copy(f32[512,7]{0,1:T(8,128)} %bitcast.7) | data formatting | bytes 28672

commit v5 on v4

--- a/solution.py
+++ b/solution.py
@@ -18,10 +18,11 @@
 F32 = jnp.float32
 
 
-UNITS = (((0, 0), (0, 1)), ((2, 0), (1, 0)), ((2, 1), (1, 1)), ((0, 2), (0, 3)), ((2, 2), (1, 2)), ((2, 3), (1, 3)))
+UNITS = (((2, 0), (1, 0)), ((0, 0), (0, 1)), ((0, 2), (0, 3)), ((2, 1), (1, 1)), ((2, 2), (1, 2)), ((2, 3), (1, 3)))
 OWN = 6
 OWN_EARLY = 3
 RING = 6
+PENDING = ((34, 0), (35, 1), (44, 2))
 Q = 128
 
 
@@ -65,7 +66,7 @@
     x_v, ws1, wn1, ids_in, mask_in, ws2, wn2, ws3t, wn3t,
     w1t, w2st, w2nt, yown, yrecv, ysum, sown, ssend, srecv,
     ids_pkt, ids_rcv, ids_s32, row_ids, idb, wb, inv,
-    ring, a_own, acc, zbase, rs_send, rs_recv, h1, h2,
+    ring, a_own, acc, zbase, pend, rs_send, via, rs_recv, h1, h2,
     in_sem, x_sem, ids_ss, ids_rs, y_ss, y_rs, s_ss, s_rs, r_ss, r_rs, g1_ss, g1_rs, g2_ss, g2_rs,
 ):
     me = lax.axis_index("g")
@@ -74,8 +75,8 @@
     cy = me // 4
     partner = me + 1 - 2 * core
     steps = (6 - 4 * cx - 8 * cy, 4 - 8 * cy, 2 - 4 * cx)
-    peers = tuple(partner + step for step in steps)
-    mates = tuple(me + step for step in steps)
+    peers = (me + steps[0], partner + steps[1], partner + steps[2])
+    mates = (partner + steps[0], me + steps[1], me + steps[2])
     mine, theirs = (me, *peers), (partner, *mates)
 
     barrier = pltpu.get_barrier_semaphore()
@@ -90,17 +91,18 @@
     ids_cp = fetch(ids_hbm, ids_in, 0)
     mask_cp = fetch(mask_hbm, mask_in, 1)
     w1_cps = [fetch(ws1_hbm, ws1, 2), fetch(wn1_hbm, wn1, 3)]
-    x_copies = []
     for b in range(N_DEV):
-        cp = pltpu.make_async_copy(x_hbm.at[:, pl.ds(b * BLK, BLK)], x_v.at[b], x_sem.at[b])
+        cp = pltpu.make_async_copy(x_hbm.at[:, pl.ds(b * BLK, BLK)], x_v.at[b], x_sem)
         cp.start()
-        x_copies.append(cp)
     late_cps = [fetch(ws2_hbm, ws2, 4), fetch(wn2_hbm, wn2, 5), fetch(ws3_hbm, ws3t, 6), fetch(wn3_hbm, wn3t, 7)]
 
     def remote(src, dst, ss, rs, dev):
         return pltpu.make_async_remote_copy(
             src_ref=src, dst_ref=dst, send_sem=ss, recv_sem=rs, device_id=(dev,), device_id_type=MESH
         )
+
+    def drain(ref, sem):
+        pltpu.make_async_copy(ref, ref, sem).wait()
 
     row_shape = (TILE // 8, 8, LANES)
     row_base = lax.broadcasted_iota(jnp.int32, row_shape, 0) * 8 + lax.broadcasted_iota(jnp.int32, row_shape, 1)
@@ -120,11 +122,9 @@
     w1t[HID:, :] = wn1[...].T
 
     pl.semaphore_wait(barrier, 4)
-    sends = []
-    id_copies = [remote(ids_pkt, ids_rcv.at[s], ids_ss.at[s], ids_rs.at[s], peers[s]) for s in range(3)]
+    id_copies = [remote(ids_pkt, ids_rcv.at[s], ids_ss, ids_rs.at[s], peers[s]) for s in range(3)]
     for cp in id_copies:
         cp.start()
-    sends += id_copies
 
     def build_own(tile):
         def put(half, g):
@@ -138,9 +138,7 @@
         for g in range(2):
             build_tile(tile, row_ids, idb, wb, OWN + g, put(0, g), put(1, g))
 
-    for cp in x_copies:
-        cp.wait()
-    y_copies, s_copies = [], []
+    drain(x_v, x_sem)
     for i in range(4):
         part = jnp.dot(w1t[...], x_v[theirs[i]], preferred_element_type=F32)
         yown[theirs[i]] = part[HID:].astype(BF)
@@ -148,15 +146,12 @@
         part2 = jnp.dot(w1t[...], x_v[mine[i]], preferred_element_type=F32)
         yown[mine[i]] = part2[HID:].astype(BF)
         sown[i] = part2[:HID]
-        for j, b in enumerate((theirs[i], mine[i])):
-            y_copies.append(remote(yown.at[b], yrecv.at[b], y_ss.at[2 * i + j], y_rs.at[2 * i + j], partner))
-            y_copies[-1].start()
-        s_copies.append(remote(ssend.at[i], srecv.at[i], s_ss.at[i], s_rs.at[i], partner))
+        for b in (theirs[i], mine[i]):
+            remote(yown.at[b], yrecv.at[b], y_ss, y_rs, partner).start()
         if i < OWN_EARLY:
             build_own(i)
-    for cp in s_copies:
-        cp.start()
-    sends += y_copies + s_copies
+    for i in range(4):
+        remote(ssend.at[i], srecv.at[i], s_ss, s_rs, partner).start()
     for tile in range(OWN_EARLY, 8):
         build_own(tile)
     for cp in late_cps:
@@ -197,46 +192,100 @@
                     ids_s32[u, :, quarter(half)] = ids_rcv[s, :, quarter(q)].astype(jnp.int32)
 
     rs_copies = {}
-    started1 = []
+
+    def rs_start(s, q, part):
+        rs_send[s, q] = part.astype(BF)
+        if s == 0:
+            copy = remote(rs_send.at[0, q], via.at[q], r_ss, r_rs.at[q], peers[1 if q % 2 else 2])
+        else:
+            copy = remote(rs_send.at[s, q], rs_recv.at[s - 1, q], r_ss, r_rs.at[4 * s + q], peers[s])
+        rs_copies[s, q] = copy
+        copy.start()
+
+    def via_slot(q):
+        return 2 if q % 2 else 1
 
     def finish_unit(u, low, high):
         total = (low * 16.0 + high) * jnp.broadcast_to(inv[u, 0:1, :], (HID, LANES))
         for half, (s, q) in enumerate(UNITS[u]):
             part = total[:, quarter(half)] + sown[1 + s, :, quarter(q)] + srecv[1 + s, :, quarter(q)].astype(F32)
-            rs_send[s, q] = part.astype(BF)
-            rs_copies[s, q] = remote(rs_send.at[s, q], rs_recv.at[s, q], r_ss.at[4 * s + q], r_rs.at[4 * s + q], peers[s])
-            rs_copies[s, q].start()
-
-    def gather_start(h, ss, rs, p):
-        outs = [remote(h.at[me, p], h.at[me, p], ss.at[7 * p + t], rs.at[7 * p + t], peers[t]) for t in range(3)]
-        outs.append(remote(h.at[me, p], h.at[me, p], ss.at[7 * p + 3], rs.at[7 * p + 3], partner))
-        for cp in outs:
-            cp.start()
-        return outs
-
-    def finish_quarter(q):
-        z = zbase[q // 2, :, quarter(q % 2)]
-        for t in (1, 2, 0):
-            rs_copies[t, q].wait_recv()
-            z = z + rs_recv[t, q].astype(F32)
-        h1[me, q] = jnp.maximum(z, 0.0).astype(BF)
-        started1.append(gather_start(h1, g1_ss, g1_rs, q))
+            if s == via_slot(q):
+                pend[q] = part
+            else:
+                rs_start(s, q, part)
+
+    def finish_pending(q):
+        rs_copies[0, q].wait_recv()
+        rs_start(via_slot(q), q, pend[q] + via[q].astype(F32))
 
     def own_base(g, own):
         base = own * jnp.broadcast_to(inv[OWN + g, 0:1, :], (HID, LANES))
         zbase[g] = base + sown[0, :, lanes(g)] + srecv[0, :, lanes(g)].astype(F32)
 
-    take_ids(0)
+    def own_dot(h, b, p):
+        rows = a_own[b, p * Q // 8 : (p + 1) * Q // 8].reshape(Q, BLK)
+        return jnp.dot(h[b, p], rows, preferred_element_type=F32)
+
+    class Gather:
+        def __init__(self, h, ss, rs, direct):
+            self.h, self.ss, self.rs, self.direct = h, ss, rs, direct
+            self.copies, self.forwards, self.ready = {}, [], []
+
+        def copy(self, block, p, slot, dev):
+            return remote(self.h.at[block, p], self.h.at[block, p], self.ss, self.rs.at[7 * p + slot], dev)
+
+        def send(self, slot, p):
+            dev = partner if slot == 3 else peers[slot]
+            self.copies[slot, p] = self.copy(me, p, slot, dev)
+            self.copies[slot, p].start()
+
+        def take(self, slot, p):
+            self.copies[slot, p].wait_recv()
+            block = partner if slot == 3 else peers[slot]
+            if p not in self.direct and slot == (1 if p % 2 else 2):
+                self.copies[0, p] = self.copy(block, p, 0, peers[3 - slot])
+                self.copies[0, p].start()
+            if slot < 3:
+                fwd = self.copy(block, p, 4 + slot, partner)
+                fwd.start()
+                self.forwards.append((slot, p, fwd))
+            self.ready.append((block, p))
+
+        def take_forwards(self, n):
+            for slot, p, fwd in self.forwards[:n]:
+                fwd.wait_recv()
+                self.ready.append((mates[slot], p))
+            self.forwards = self.forwards[n:]
+
+        def own(self, pieces):
+            acc[...] = sum(own_dot(self.h, me, p) for p in range(pieces))
+
+        def add(self):
+            acc[...] += sum(own_dot(self.h, b, p) for b, p in self.ready)
+            self.ready = []
+
+    g1 = Gather(h1, g1_ss, g1_rs, direct=(3,))
+    g2 = Gather(h2, g2_ss, g2_rs, direct=())
+
+    def finish_quarter(q):
+        z = zbase[q // 2, :, quarter(q % 2)]
+        for t in (1, 2):
+            rs_copies[t, q].wait_recv()
+            z = z + rs_recv[t - 1, q].astype(F32)
+        h1[me, q] = jnp.maximum(z, 0.0).astype(BF)
+        for slot in (0, 2, 1, 3) if q in g1.direct else (2, 1, 3):
+            g1.send(slot, q)
+
+    take_ids(2)
+    take_ids(1)
     spread_ids(ids_s32, idb, wb, inv, 0)
     lead = 3
     for flat in range(lead):
         build_into(flat)
-    for cp in y_copies:
-        cp.wait_recv()
+    drain(yrecv, y_rs)
     for b in range(N_DEV):
         ysum[b] = yown[b] + yrecv[b]
-    take_ids(2)
-    take_ids(1)
+    take_ids(0)
     built = lead
     low = high = own = None
     for flat in range(48):
@@ -254,86 +303,102 @@
             own = piece if own is None else own + piece
         if tile == 7:
             if u == 0:
-                for cp in s_copies:
-                    cp.wait_recv()
+                drain(srecv, s_rs)
             finish_unit(u, low, high)
             low = high = None
             if u in (1, 3):
                 own_base(u // 2, own)
                 own = None
-            if u == 4:
-                finish_quarter(0)
+        for when, q in PENDING:
+            if flat == when:
+                finish_pending(q)
+    finish_pending(3)
+    finish_quarter(0)
     finish_quarter(1)
     finish_quarter(2)
+    g1.own(3)
+    g1.take(2, 0)
+    g1.take(1, 0)
     finish_quarter(3)
-    sends += list(rs_copies.values())
+    g1.ready.append((me, 3))
+    for slot, p in ((1, 1), (2, 1), (2, 2), (1, 2)):
+        g1.take(slot, p)
+    for p in range(4):
+        g1.take(3, p)
+    g1.add()
+    g1.take(0, 0)
+    g1.take(0, 1)
+    g1.take_forwards(6)
+    g1.add()
+    for slot, p in ((2, 3), (1, 3), (0, 3), (0, 2)):
+        g1.take(slot, p)
+    g1.add()
+    g1.take_forwards(4)
+    g1.add()
+    g1.take_forwards(2)
+    g1.add()
 
     inv_own = jnp.concatenate(
         [jnp.broadcast_to(inv[OWN + g, 0:1, :], (HID, LANES)) for g in range(2)], axis=1
     )
-
-    def own_dot(h, b, p, size):
-        rows = a_own[b, p * size // 8 : (p + 1) * size // 8].reshape(size, BLK)
-        return jnp.dot(h[b, p], rows, preferred_element_type=F32)
-
-    def gather_finish(h, ss, rs, started, size, old_sends):
-        pieces = BLK // size
-        acc[...] = sum(own_dot(h, me, p, size) for p in range(pieces))
-        for cp in old_sends:
-            cp.wait_send()
-        forwards = []
-
-        def take_forwards(p):
-            for fwd in forwards[p]:
-                fwd.wait_recv()
-            acc[...] += sum(own_dot(h, mate, p, size) for mate in mates)
-
-        for p in range(pieces):
-            group = []
-            for t in (1, 2, 0):
-                started[p][t].wait_recv()
-                fwd = remote(
-                    h.at[peers[t], p], h.at[peers[t], p], ss.at[7 * p + 4 + t], rs.at[7 * p + 4 + t], partner
-                )
-                fwd.start()
-                group.append(fwd)
-            forwards.append(group)
-            started[p][3].wait_recv()
-            acc[...] += sum(own_dot(h, dev, p, size) for dev in (*peers, partner))
-            if p > 0:
-                take_forwards(p - 1)
-        take_forwards(pieces - 1)
-        return [cp for outs in started for cp in outs] + [cp for group in forwards for cp in group]
-
-    sends = gather_finish(h1, g1_ss, g1_rs, started1, Q, sends)
-
-    started2 = []
     for g in range(2):
         mean1 = (acc[:, lanes(g)] * inv_own[:, lanes(g)]).astype(BF)
-        mine = jnp.concatenate([h1[me, 2 * g], h1[me, 2 * g + 1]], axis=1)
-        pre2 = jnp.dot(w2st[...], mine, preferred_element_type=F32) + jnp.dot(
+        block = jnp.concatenate([h1[me, 2 * g], h1[me, 2 * g + 1]], axis=1)
+        pre2 = jnp.dot(w2st[...], block, preferred_element_type=F32) + jnp.dot(
             w2nt[...], mean1, preferred_element_type=F32
         )
-        h2[me, g] = jnp.maximum(pre2, 0.0).astype(BF)
-        started2.append(gather_start(h2, g2_ss, g2_rs, g))
+        for half in range(2):
+            h2[me, 2 * g + half] = jnp.maximum(pre2[:, quarter(half)], 0.0).astype(BF)
+        g2.send(2, 2 * g)
+        g2.send(1, 2 * g + 1)
+    for slot, p in ((2, 1), (1, 0), (2, 3), (1, 2)):
+        g2.send(slot, p)
+    for p in range(4):
+        g2.send(3, p)
+    g2.own(4)
     for g in range(2):
-        out_ref[:, lanes(g)] = jnp.dot(ws3t[...], h2[me, g], preferred_element_type=F32)
-    sends = gather_finish(h2, g2_ss, g2_rs, started2, LANES, sends)
+        block = jnp.concatenate([h2[me, 2 * g], h2[me, 2 * g + 1]], axis=1)
+        out_ref[:, lanes(g)] = jnp.dot(ws3t[...], block, preferred_element_type=F32)
+    drain(ids_rcv, ids_ss)
+    drain(yown, y_ss)
+    drain(ssend, s_ss)
+    drain(rs_send, r_ss)
+    drain(h1.at[0:7], g1_ss)
+    for p in range(4):
+        g2.take(3, p)
+    g2.add()
+    for slot, p in ((2, 0), (1, 1), (2, 2), (1, 3)):
+        g2.take(slot, p)
+    g2.add()
+    for slot, p in ((2, 1), (1, 0), (2, 3), (1, 2)):
+        g2.take(slot, p)
+    g2.take_forwards(4)
+    g2.add()
+    g2.take(0, 0)
+    g2.take(0, 1)
+    g2.take_forwards(4)
+    g2.add()
+    g2.take(0, 2)
+    g2.take(0, 3)
+    g2.take_forwards(2)
+    g2.add()
+    g2.take_forwards(2)
+    g2.add()
     for g in range(2):
         mean2 = (acc[:, lanes(g)] * inv_own[:, lanes(g)]).astype(BF)
         out_ref[:, lanes(g)] += jnp.dot(wn3t[...], mean2, preferred_element_type=F32)
-    for cp in sends:
-        cp.wait_send()
+    drain(h2.at[0:7], g2_ss)
 
 
 def solution(mesh):
     def device_step(feat, ws1, wn1, ids, mask, ws2, wn2, ws3, wn3):
+        operands = (feat.T, ws1, wn1, ids.T, mask.T, ws2, wn2, ws3.T, wn3.T)
         vm = pl.BlockSpec(memory_space=pltpu.VMEM)
         dma = pltpu.SemaphoreType.DMA
         out_t = pl.pallas_call(
             kernel,
             out_shape=jax.ShapeDtypeStruct((7, BLK), F32),
-            in_specs=[pl.BlockSpec(memory_space=pl.ANY)] * 9,
+            in_specs=[pl.BlockSpec(memory_space=pltpu.HBM)] * 9,
             out_specs=vm,
             scratch_shapes=[
                 pltpu.VMEM((N_DEV, 192, BLK), BF),
@@ -365,24 +430,26 @@
                 pltpu.VMEM((N_DEV, BLK // 8, 8, BLK), BF),
                 pltpu.VMEM((HID, BLK), F32),
                 pltpu.VMEM((2, HID, LANES), F32),
+                pltpu.VMEM((4, HID, Q), F32),
                 pltpu.VMEM((3, 4, HID, Q), BF),
-                pltpu.VMEM((3, 4, HID, Q), BF),
+                pltpu.VMEM((4, HID, Q), BF),
+                pltpu.VMEM((2, 4, HID, Q), BF),
                 pltpu.VMEM((N_DEV, 4, HID, Q), BF),
-                pltpu.VMEM((N_DEV, 2, HID, LANES), BF),
+                pltpu.VMEM((N_DEV, 4, HID, Q), BF),
                 dma((8,)),
-                dma((N_DEV,)),
-                dma((3,)), dma((3,)),
-                dma((8,)), dma((8,)),
-                dma((4,)), dma((4,)),
-                dma((12,)), dma((12,)),
-                dma((28,)), dma((28,)),
-                dma((14,)), dma((14,)),
+                dma,
+                dma, dma((3,)),
+                dma, dma,
+                dma, dma,
+                dma, dma((12,)),
+                dma, dma((28,)),
+                dma, dma((28,)),
             ],
             compiler_params=pltpu.CompilerParams(
-                collective_id=0, has_side_effects=True, vmem_limit_bytes=60 * 1024 * 1024
+                collective_id=0, has_side_effects=True, vmem_limit_bytes=32 * 1024 * 1024
             ),
             name="graphsage",
-        )(feat.T, ws1, wn1, ids.T, mask.T, ws2, wn2, ws3.T, wn3.T)
+        )(*(pltpu.with_memory_space_constraint(a, pltpu.HBM) for a in operands))
         return out_t.T
 
     col_split = P(None, "g")

time: 36.6 us -> 33.6 us (0.918)
  Pallas kernels: 35.1 us -> 32.9 us
  local copies, waits for them, and re-layouts: 1.32 us -> 0.61 us
    pallas_call x1, Pallas kernels: 35.1 us -> 32.9 us  [device_step(): pl.pallas_call(kernel, out_shape=jax.ShapeDtypeStruct((7, BLK), F32), in_...]
    unnamed x1, local copies, waits for them, and re-layouts: 1.32 us -> 0.61 us
where the time goes in v5:
time: 33.6 us; the launch traced here: 33.5 us
  Pallas kernels  32.9 us (98%)
  local copies, waits for them, and re-layouts  0.61 us (2%)
    pallas_call x1, Pallas kernels, device_step(): pl.pallas_call(kernel, out_shape=jax.ShapeDtypeStruct((7, BLK), F32), in_...  32.9 us

profile of v5, /device:TPU:0, one launch (start us, length us, event | category | flops | bytes accessed | tf_op | source)
XLA Modules:
  0.0 33.5 jit_solution(4630795690039377318)
XLA Ops:
  0.0 32.9 %graphsage.1 = f32[7,512]{1,0:T(8,128)S(1)} custom-call(bf16[192,4096]{1,0:T(8,128)(2,1)} %bitcast.7, bf16[192,128]{1,0:T(8,128)(2,1)} %ws1_hbm.1, bf16[192,128]{1,0:T(8,128)(2,1)} %wn1_hbm.1, s32[10,512]{1,0:T(8,128)} %bitcast.8, s32[10,512]{1,0:T(8,128)} %bitcast.9, bf16[128,128]{1,0:T(8,128)(2,1)} %ws2_hbm.1, bf16[128,128]{1,0:T(8,128)(2,1)} %wn2_hbm.1, ...), custom_call_target="tpu_custom_call" | custom-call | tf_op jit(solution)/shard_map/graphsage/pallas_call | solution.py:398
  32.9 0.6 %copy.11 = f32[512,7]{0,1:T(8,128)} copy(f32[512,7]{0,1:T(8,128)S(1)} %bitcast.6) | data formatting | bytes 28672

commit v6 on v5

--- a/solution.py
+++ b/solution.py
@@ -18,11 +18,11 @@
 F32 = jnp.float32
 
 
-UNITS = (((2, 0), (1, 0)), ((0, 0), (0, 1)), ((0, 2), (0, 3)), ((2, 1), (1, 1)), ((2, 2), (1, 2)), ((2, 3), (1, 3)))
+UNITS = (((2, 2), (1, 2)), ((0, 0), (0, 1)), ((0, 2), (0, 3)), ((2, 0), (1, 0)), ((2, 1), (1, 1)), ((2, 3), (1, 3)))
 OWN = 6
 OWN_EARLY = 3
 RING = 6
-PENDING = ((34, 0), (35, 1), (44, 2))
+PENDING = ((40, 0), (41, 1), (47, 2), (47, 3))
 Q = 128
 
 
@@ -285,12 +285,13 @@
     drain(yrecv, y_rs)
     for b in range(N_DEV):
         ysum[b] = yown[b] + yrecv[b]
-    take_ids(0)
     built = lead
     low = high = own = None
     for flat in range(48):
         u, tile = flat // 8, flat % 8
         while built < 48 and built - flat < 2 or (built < 48 and tile % 2 == 0 and built - flat < lead):
+            if built == 8:
+                take_ids(0)
             if built % 8 == 0:
                 spread_ids(ids_s32, idb, wb, inv, built // 8)
             build_into(built)
@@ -312,16 +313,12 @@
         for when, q in PENDING:
             if flat == when:
                 finish_pending(q)
-    finish_pending(3)
     finish_quarter(0)
     finish_quarter(1)
     finish_quarter(2)
-    g1.own(3)
-    g1.take(2, 0)
-    g1.take(1, 0)
     finish_quarter(3)
-    g1.ready.append((me, 3))
-    for slot, p in ((1, 1), (2, 1), (2, 2), (1, 2)):
+    g1.own(4)
+    for slot, p in ((2, 0), (1, 0), (1, 1), (2, 1), (2, 2), (1, 2)):
         g1.take(slot, p)
     for p in range(4):
         g1.take(3, p)

time: 33.6 us -> 33.5 us (level)
  no operation moved by 1% of the time
where the time goes in v6:
time: 33.5 us; the launch traced here: 33.4 us
  Pallas kernels  32.8 us (98%)
  local copies, waits for them, and re-layouts  0.61 us (2%)
    pallas_call x1, Pallas kernels, device_step(): pl.pallas_call(kernel, out_shape=jax.ShapeDtypeStruct((7, BLK), F32), in_...  32.8 us

profile of v6, /device:TPU:0, one launch (start us, length us, event | category | flops | bytes accessed | tf_op | source)
XLA Modules:
  0.0 33.4 jit_solution(11159220372079085298)
XLA Ops:
  0.0 32.8 %graphsage.1 = f32[7,512]{1,0:T(8,128)S(1)} custom-call(bf16[192,4096]{1,0:T(8,128)(2,1)} %bitcast.7, bf16[192,128]{1,0:T(8,128)(2,1)} %ws1_hbm.1, bf16[192,128]{1,0:T(8,128)(2,1)} %wn1_hbm.1, s32[10,512]{1,0:T(8,128)} %bitcast.8, s32[10,512]{1,0:T(8,128)} %bitcast.9, bf16[128,128]{1,0:T(8,128)(2,1)} %ws2_hbm.1, bf16[128,128]{1,0:T(8,128)(2,1)} %wn2_hbm.1, ...), custom_call_target="tpu_custom_call" | custom-call | tf_op jit(solution)/shard_map/graphsage/pallas_call | solution.py:395
  32.8 0.6 %copy.11 = f32[512,7]{0,1:T(8,128)} copy(f32[512,7]{0,1:T(8,128)S(1)} %bitcast.6) | data formatting | bytes 28672

commit v7 on v6

--- a/solution.py
+++ b/solution.py
@@ -18,11 +18,10 @@
 F32 = jnp.float32
 
 
-UNITS = (((2, 2), (1, 2)), ((0, 0), (0, 1)), ((0, 2), (0, 3)), ((2, 0), (1, 0)), ((2, 1), (1, 1)), ((2, 3), (1, 3)))
+UNITS = (((2, 0), (1, 0)), ((0, 0), (0, 1)), ((2, 1), (1, 1)), ((0, 2), (0, 3)), ((2, 2), (1, 2)), ((2, 3), (1, 3)))
 OWN = 6
 OWN_EARLY = 3
 RING = 6
-PENDING = ((40, 0), (41, 1), (47, 2), (47, 3))
 Q = 128
 
 
@@ -66,7 +65,7 @@
     x_v, ws1, wn1, ids_in, mask_in, ws2, wn2, ws3t, wn3t,
     w1t, w2st, w2nt, yown, yrecv, ysum, sown, ssend, srecv,
     ids_pkt, ids_rcv, ids_s32, row_ids, idb, wb, inv,
-    ring, a_own, acc, zbase, pend, rs_send, via, rs_recv, h1, h2,
+    ring, a_own, acc, zbase, rs_send, rs_recv, h1, h2,
     in_sem, x_sem, ids_ss, ids_rs, y_ss, y_rs, s_ss, s_rs, r_ss, r_rs, g1_ss, g1_rs, g2_ss, g2_rs,
 ):
     me = lax.axis_index("g")
@@ -75,8 +74,8 @@
     cy = me // 4
     partner = me + 1 - 2 * core
     steps = (6 - 4 * cx - 8 * cy, 4 - 8 * cy, 2 - 4 * cx)
-    peers = (me + steps[0], partner + steps[1], partner + steps[2])
-    mates = (partner + steps[0], me + steps[1], me + steps[2])
+    peers = tuple(partner + step for step in steps)
+    mates = tuple(me + step for step in steps)
     mine, theirs = (me, *peers), (partner, *mates)
 
     barrier = pltpu.get_barrier_semaphore()
@@ -193,30 +192,13 @@
 
     rs_copies = {}
 
-    def rs_start(s, q, part):
-        rs_send[s, q] = part.astype(BF)
-        if s == 0:
-            copy = remote(rs_send.at[0, q], via.at[q], r_ss, r_rs.at[q], peers[1 if q % 2 else 2])
-        else:
-            copy = remote(rs_send.at[s, q], rs_recv.at[s - 1, q], r_ss, r_rs.at[4 * s + q], peers[s])
-        rs_copies[s, q] = copy
-        copy.start()
-
-    def via_slot(q):
-        return 2 if q % 2 else 1
-
     def finish_unit(u, low, high):
         total = (low * 16.0 + high) * jnp.broadcast_to(inv[u, 0:1, :], (HID, LANES))
         for half, (s, q) in enumerate(UNITS[u]):
             part = total[:, quarter(half)] + sown[1 + s, :, quarter(q)] + srecv[1 + s, :, quarter(q)].astype(F32)
-            if s == via_slot(q):
-                pend[q] = part
-            else:
-                rs_start(s, q, part)
-
-    def finish_pending(q):
-        rs_copies[0, q].wait_recv()
-        rs_start(via_slot(q), q, pend[q] + via[q].astype(F32))
+            rs_send[s, q] = part.astype(BF)
+            rs_copies[s, q] = remote(rs_send.at[s, q], rs_recv.at[s, q], r_ss, r_rs.at[4 * s + q], peers[s])
+            rs_copies[s, q].start()
 
     def own_base(g, own):
         base = own * jnp.broadcast_to(inv[OWN + g, 0:1, :], (HID, LANES))
@@ -241,7 +223,7 @@
 
         def take(self, slot, p):
             self.copies[slot, p].wait_recv()
-            block = partner if slot == 3 else peers[slot]
+            block = partner if slot == 3 else mates[0] if slot == 0 and p not in self.direct else peers[slot]
             if p not in self.direct and slot == (1 if p % 2 else 2):
                 self.copies[0, p] = self.copy(block, p, 0, peers[3 - slot])
                 self.copies[0, p].start()
@@ -254,7 +236,8 @@
         def take_forwards(self, n):
             for slot, p, fwd in self.forwards[:n]:
                 fwd.wait_recv()
-                self.ready.append((mates[slot], p))
+                relayed = slot == 0 and p not in self.direct
+                self.ready.append((peers[0] if relayed else mates[slot], p))
             self.forwards = self.forwards[n:]
 
         def own(self, pieces):
@@ -269,9 +252,9 @@
 
     def finish_quarter(q):
         z = zbase[q // 2, :, quarter(q % 2)]
-        for t in (1, 2):
+        for t in (1, 2, 0):
             rs_copies[t, q].wait_recv()
-            z = z + rs_recv[t - 1, q].astype(F32)
+            z = z + rs_recv[t, q].astype(F32)
         h1[me, q] = jnp.maximum(z, 0.0).astype(BF)
         for slot in (0, 2, 1, 3) if q in g1.direct else (2, 1, 3):
             g1.send(slot, q)
@@ -310,9 +293,6 @@
             if u in (1, 3):
                 own_base(u // 2, own)
                 own = None
-        for when, q in PENDING:
-            if flat == when:
-                finish_pending(q)
     finish_quarter(0)
     finish_quarter(1)
     finish_quarter(2)
@@ -427,10 +407,8 @@
                 pltpu.VMEM((N_DEV, BLK // 8, 8, BLK), BF),
                 pltpu.VMEM((HID, BLK), F32),
                 pltpu.VMEM((2, HID, LANES), F32),
-                pltpu.VMEM((4, HID, Q), F32),
                 pltpu.VMEM((3, 4, HID, Q), BF),
-                pltpu.VMEM((4, HID, Q), BF),
-                pltpu.VMEM((2, 4, HID, Q), BF),
+                pltpu.VMEM((3, 4, HID, Q), BF),
                 pltpu.VMEM((N_DEV, 4, HID, Q), BF),
                 pltpu.VMEM((N_DEV, 4, HID, Q), BF),
                 dma((8,)),

time: 33.5 us -> 33 us (0.985)
  Pallas kernels: 32.8 us -> 32.3 us
    pallas_call x1, Pallas kernels: 32.8 us -> 32.3 us  [device_step(): pl.pallas_call(kernel, out_shape=jax.ShapeDtypeStruct((7, BLK), F32), in_...]
where the time goes in v7:
time: 33 us; the launch traced here: 32.9 us
  Pallas kernels  32.3 us (98%)
  local copies, waits for them, and re-layouts  0.61 us (2%)
    pallas_call x1, Pallas kernels, device_step(): pl.pallas_call(kernel, out_shape=jax.ShapeDtypeStruct((7, BLK), F32), in_...  32.3 us

profile of v7, /device:TPU:0, one launch (start us, length us, event | category | flops | bytes accessed | tf_op | source)
XLA Modules:
  0.0 32.9 jit_solution(4689545849806944895)
XLA Ops:
  0.0 32.3 %graphsage.1 = f32[7,512]{1,0:T(8,128)S(1)} custom-call(bf16[192,4096]{1,0:T(8,128)(2,1)} %bitcast.7, bf16[192,128]{1,0:T(8,128)(2,1)} %ws1_hbm.1, bf16[192,128]{1,0:T(8,128)(2,1)} %wn1_hbm.1, s32[10,512]{1,0:T(8,128)} %bitcast.8, s32[10,512]{1,0:T(8,128)} %bitcast.9, bf16[128,128]{1,0:T(8,128)(2,1)} %ws2_hbm.1, bf16[128,128]{1,0:T(8,128)(2,1)} %wn2_hbm.1, ...), custom_call_target="tpu_custom_call" | custom-call | tf_op jit(solution)/shard_map/graphsage/pallas_call | solution.py:375
  32.3 0.6 %copy.11 = f32[512,7]{0,1:T(8,128)} copy(f32[512,7]{0,1:T(8,128)S(1)} %bitcast.6) | data formatting | bytes 28672

commit v8 on v7

--- a/solution.py
+++ b/solution.py
@@ -295,10 +295,14 @@
                 own = None
     finish_quarter(0)
     finish_quarter(1)
+    g1.take(2, 0)
+    g1.take(1, 0)
     finish_quarter(2)
+    g1.take(1, 1)
+    g1.take(2, 1)
     finish_quarter(3)
     g1.own(4)
-    for slot, p in ((2, 0), (1, 0), (1, 1), (2, 1), (2, 2), (1, 2)):
+    for slot, p in ((2, 2), (1, 2)):
         g1.take(slot, p)
     for p in range(4):
         g1.take(3, p)

time: 33 us -> 34.3 us (1.039)
  Pallas kernels: 32.3 us -> 33.6 us
    pallas_call x1, Pallas kernels: 32.3 us -> 33.6 us  [device_step(): pl.pallas_call(kernel, out_shape=jax.ShapeDtypeStruct((7, BLK), F32), in_...]
where the time goes in v8:
time: 34.3 us; the launch traced here: 34.2 us
  Pallas kernels  33.6 us (98%)
  local copies, waits for them, and re-layouts  0.61 us (2%)
    pallas_call x1, Pallas kernels, device_step(): pl.pallas_call(kernel, out_shape=jax.ShapeDtypeStruct((7, BLK), F32), in_...  33.6 us

profile of v8, /device:TPU:0, one launch (start us, length us, event | category | flops | bytes accessed | tf_op | source)
XLA Modules:
  0.0 34.2 jit_solution(16590034365828027579)
XLA Ops:
  0.0 33.6 %graphsage.1 = f32[7,512]{1,0:T(8,128)S(1)} custom-call(bf16[192,4096]{1,0:T(8,128)(2,1)} %bitcast.7, bf16[192,128]{1,0:T(8,128)(2,1)} %ws1_hbm.1, bf16[192,128]{1,0:T(8,128)(2,1)} %wn1_hbm.1, s32[10,512]{1,0:T(8,128)} %bitcast.8, s32[10,512]{1,0:T(8,128)} %bitcast.9, bf16[128,128]{1,0:T(8,128)(2,1)} %ws2_hbm.1, bf16[128,128]{1,0:T(8,128)(2,1)} %wn2_hbm.1, ...), custom_call_target="tpu_custom_call" | custom-call | tf_op jit(solution)/shard_map/graphsage/pallas_call | solution.py:379
  33.6 0.6 %copy.11 = f32[512,7]{0,1:T(8,128)} copy(f32[512,7]{0,1:T(8,128)S(1)} %bitcast.6) | data formatting | bytes 28672

commit v9 on v7

--- a/solution.py
+++ b/solution.py
@@ -20,7 +20,6 @@
 
 UNITS = (((2, 0), (1, 0)), ((0, 0), (0, 1)), ((2, 1), (1, 1)), ((0, 2), (0, 3)), ((2, 2), (1, 2)), ((2, 3), (1, 3)))
 OWN = 6
-OWN_EARLY = 3
 RING = 6
 Q = 128
 
@@ -112,6 +111,10 @@
     mask_cp.wait()
     masked = jnp.where(mask_in[...] > 0, ids_in[...], -1)
     ids_pkt[0:FAN, :] = masked.astype(jnp.int16)
+    pl.semaphore_wait(barrier, 4)
+    id_copies = [remote(ids_pkt, ids_rcv.at[s], ids_ss, ids_rs.at[s], peers[s]) for s in range(3)]
+    for s in (2, 1, 0):
+        id_copies[s].start()
     for g in range(2):
         ids_s32[OWN + g, 0:FAN, :] = masked[:, g * LANES : (g + 1) * LANES]
         spread_ids(ids_s32, idb, wb, inv, OWN + g)
@@ -120,13 +123,8 @@
     w1t[0:HID, :] = ws1[...].T
     w1t[HID:, :] = wn1[...].T
 
-    pl.semaphore_wait(barrier, 4)
-    id_copies = [remote(ids_pkt, ids_rcv.at[s], ids_ss, ids_rs.at[s], peers[s]) for s in range(3)]
-    for cp in id_copies:
-        cp.start()
-
-    def build_own(tile):
-        def put(half, g):
+    def build_own(tile, g):
+        def put(half):
             def store(r, v):
                 v = v if half else v * jnp.array(16.0, BF)
                 row = tile % 2 * (TILE // 8) + r
@@ -134,8 +132,7 @@
 
             return store
 
-        for g in range(2):
-            build_tile(tile, row_ids, idb, wb, OWN + g, put(0, g), put(1, g))
+        build_tile(tile, row_ids, idb, wb, OWN + g, put(0), put(1))
 
     drain(x_v, x_sem)
     for i in range(4):
@@ -147,12 +144,11 @@
         sown[i] = part2[:HID]
         for b in (theirs[i], mine[i]):
             remote(yown.at[b], yrecv.at[b], y_ss, y_rs, partner).start()
-        if i < OWN_EARLY:
-            build_own(i)
+        build_own(2 * i, 0)
     for i in range(4):
         remote(ssend.at[i], srecv.at[i], s_ss, s_rs, partner).start()
-    for tile in range(OWN_EARLY, 8):
-        build_own(tile)
+    for tile in range(1, 8, 2):
+        build_own(tile, 0)
     for cp in late_cps:
         cp.wait()
     w2st[...] = ws2[...].T
@@ -199,6 +195,9 @@
             rs_send[s, q] = part.astype(BF)
             rs_copies[s, q] = remote(rs_send.at[s, q], rs_recv.at[s, q], r_ss, r_rs.at[4 * s + q], peers[s])
             rs_copies[s, q].start()
+
+    def own_piece(b, g):
+        return jnp.dot(ysum[b], a_own[b, :, :, lanes(g)].reshape(BLK, LANES), preferred_element_type=F32)
 
     def own_base(g, own):
         base = own * jnp.broadcast_to(inv[OWN + g, 0:1, :], (HID, LANES))
@@ -282,22 +281,26 @@
         part = dot_from(flat)
         low = part[0] if low is None else low + part[0]
         high = part[1] if high is None else high + part[1]
-        if u in (1, 3):
-            piece = jnp.dot(ysum[tile], a_own[tile, :, :, lanes(u // 2)].reshape(BLK, LANES), preferred_element_type=F32)
-            own = piece if own is None else own + piece
+        if u == 1:
+            own = own_piece(tile, 0) if own is None else own + own_piece(tile, 0)
         if tile == 7:
             if u == 0:
                 drain(srecv, s_rs)
             finish_unit(u, low, high)
             low = high = None
-            if u in (1, 3):
-                own_base(u // 2, own)
-                own = None
+            if u == 1:
+                own_base(0, own)
     finish_quarter(0)
     finish_quarter(1)
+    for tile in range(8):
+        build_own(tile, 1)
+    own_base(1, sum(own_piece(b, 1) for b in range(N_DEV)))
     finish_quarter(2)
     finish_quarter(3)
     g1.own(4)
+    for g in range(2):
+        block = jnp.concatenate([h1[me, 2 * g], h1[me, 2 * g + 1]], axis=1)
+        zbase[g] = jnp.dot(w2st[...], block, preferred_element_type=F32)
     for slot, p in ((2, 0), (1, 0), (1, 1), (2, 1), (2, 2), (1, 2)):
         g1.take(slot, p)
     for p in range(4):
@@ -320,10 +323,7 @@
     )
     for g in range(2):
         mean1 = (acc[:, lanes(g)] * inv_own[:, lanes(g)]).astype(BF)
-        block = jnp.concatenate([h1[me, 2 * g], h1[me, 2 * g + 1]], axis=1)
-        pre2 = jnp.dot(w2st[...], block, preferred_element_type=F32) + jnp.dot(
-            w2nt[...], mean1, preferred_element_type=F32
-        )
+        pre2 = zbase[g] + jnp.dot(w2nt[...], mean1, preferred_element_type=F32)
         for half in range(2):
             h2[me, 2 * g + half] = jnp.maximum(pre2[:, quarter(half)], 0.0).astype(BF)
         g2.send(2, 2 * g)

time: 33 us -> 33.2 us (level)
  no operation moved by 1% of the time
where the time goes in v9:
time: 33.2 us; the launch traced here: 33.1 us
  Pallas kernels  32.5 us (98%)
  local copies, waits for them, and re-layouts  0.61 us (2%)
    pallas_call x1, Pallas kernels, device_step(): pl.pallas_call(kernel, out_shape=jax.ShapeDtypeStruct((7, BLK), F32), in_...  32.5 us

profile of v9, /device:TPU:0, one launch (start us, length us, event | category | flops | bytes accessed | tf_op | source)
XLA Modules:
  0.0 33.1 jit_solution(12825869803686718302)
XLA Ops:
  0.0 32.5 %graphsage.1 = f32[7,512]{1,0:T(8,128)S(1)} custom-call(bf16[192,4096]{1,0:T(8,128)(2,1)} %bitcast.7, bf16[192,128]{1,0:T(8,128)(2,1)} %ws1_hbm.1, bf16[192,128]{1,0:T(8,128)(2,1)} %wn1_hbm.1, s32[10,512]{1,0:T(8,128)} %bitcast.8, s32[10,512]{1,0:T(8,128)} %bitcast.9, bf16[128,128]{1,0:T(8,128)(2,1)} %ws2_hbm.1, bf16[128,128]{1,0:T(8,128)(2,1)} %wn2_hbm.1, ...), custom_call_target="tpu_custom_call" | custom-call | tf_op jit(solution)/shard_map/graphsage/pallas_call | solution.py:375
  32.5 0.6 %copy.11 = f32[512,7]{0,1:T(8,128)} copy(f32[512,7]{0,1:T(8,128)S(1)} %bitcast.6) | data formatting | bytes 28672

commit v10 on v9

--- a/solution.py
+++ b/solution.py
@@ -290,10 +290,10 @@
             low = high = None
             if u == 1:
                 own_base(0, own)
+    for tile in range(8):
+        build_own(tile, 1)
     finish_quarter(0)
     finish_quarter(1)
-    for tile in range(8):
-        build_own(tile, 1)
     own_base(1, sum(own_piece(b, 1) for b in range(N_DEV)))
     finish_quarter(2)
     finish_quarter(3)

time: 33.2 us -> 33.1 us (level)
  no operation moved by 1% of the time
where the time goes in v10:
time: 33.1 us; the launch traced here: 33 us
  Pallas kernels  32.3 us (98%)
  local copies, waits for them, and re-layouts  0.61 us (2%)
    pallas_call x1, Pallas kernels, device_step(): pl.pallas_call(kernel, out_shape=jax.ShapeDtypeStruct((7, BLK), F32), in_...  32.3 us

profile of v10, /device:TPU:0, one launch (start us, length us, event | category | flops | bytes accessed | tf_op | source)
XLA Modules:
  0.0 33.0 jit_solution(345484721186820584)
XLA Ops:
  0.0 32.3 %graphsage.1 = f32[7,512]{1,0:T(8,128)S(1)} custom-call(bf16[192,4096]{1,0:T(8,128)(2,1)} %bitcast.7, bf16[192,128]{1,0:T(8,128)(2,1)} %ws1_hbm.1, bf16[192,128]{1,0:T(8,128)(2,1)} %wn1_hbm.1, s32[10,512]{1,0:T(8,128)} %bitcast.8, s32[10,512]{1,0:T(8,128)} %bitcast.9, bf16[128,128]{1,0:T(8,128)(2,1)} %ws2_hbm.1, bf16[128,128]{1,0:T(8,128)(2,1)} %wn2_hbm.1, ...), custom_call_target="tpu_custom_call" | custom-call | tf_op jit(solution)/shard_map/graphsage/pallas_call | solution.py:375
  32.4 0.6 %copy.11 = f32[512,7]{0,1:T(8,128)} copy(f32[512,7]{0,1:T(8,128)S(1)} %bitcast.6) | data formatting | bytes 28672

commit v11 on v10

--- a/solution.py
+++ b/solution.py
@@ -18,7 +18,7 @@
 F32 = jnp.float32
 
 
-UNITS = (((2, 0), (1, 0)), ((0, 0), (0, 1)), ((2, 1), (1, 1)), ((0, 2), (0, 3)), ((2, 2), (1, 2)), ((2, 3), (1, 3)))
+UNITS = (((2, 0), (1, 0)), ((2, 1), (1, 1)), ((0, 0), (0, 1)), ((0, 2), (0, 3)), ((2, 2), (1, 2)), ((2, 3), (1, 3)))
 OWN = 6
 RING = 6
 Q = 128
@@ -65,7 +65,7 @@
     w1t, w2st, w2nt, yown, yrecv, ysum, sown, ssend, srecv,
     ids_pkt, ids_rcv, ids_s32, row_ids, idb, wb, inv,
     ring, a_own, acc, zbase, rs_send, rs_recv, h1, h2,
-    in_sem, x_sem, ids_ss, ids_rs, y_ss, y_rs, s_ss, s_rs, r_ss, r_rs, g1_ss, g1_rs, g2_ss, g2_rs,
+    in_sem, x_sem, ids_ss, ids_rs, y_ss, y_rs, s_ss, s_rs, r_ss, r_rs, g1_ss, g1_rs, g2_ss, g2_rs, go_sem,
 ):
     me = lax.axis_index("g")
     core = lax.rem(me, 2)
@@ -73,12 +73,12 @@
     cy = me // 4
     partner = me + 1 - 2 * core
     steps = (6 - 4 * cx - 8 * cy, 4 - 8 * cy, 2 - 4 * cx)
-    peers = tuple(partner + step for step in steps)
-    mates = tuple(me + step for step in steps)
+    peers = (me + steps[0], partner + steps[1], partner + steps[2])
+    mates = (partner + steps[0], me + steps[1], me + steps[2])
     mine, theirs = (me, *peers), (partner, *mates)
 
     barrier = pltpu.get_barrier_semaphore()
-    for peer in (*peers, partner):
+    for peer in (peers[1], peers[2], partner):
         pl.semaphore_signal(barrier, inc=1, device_id=(peer,), device_id_type=MESH)
 
     def fetch(src, dst, i):
@@ -111,9 +111,10 @@
     mask_cp.wait()
     masked = jnp.where(mask_in[...] > 0, ids_in[...], -1)
     ids_pkt[0:FAN, :] = masked.astype(jnp.int16)
-    pl.semaphore_wait(barrier, 4)
+    pl.semaphore_wait(barrier, 3)
+    pl.semaphore_signal(go_sem, inc=1, device_id=(peers[2],), device_id_type=MESH)
     id_copies = [remote(ids_pkt, ids_rcv.at[s], ids_ss, ids_rs.at[s], peers[s]) for s in range(3)]
-    for s in (2, 1, 0):
+    for s in (2, 1):
         id_copies[s].start()
     for g in range(2):
         ids_s32[OWN + g, 0:FAN, :] = masked[:, g * LANES : (g + 1) * LANES]
@@ -145,6 +146,9 @@
         for b in (theirs[i], mine[i]):
             remote(yown.at[b], yrecv.at[b], y_ss, y_rs, partner).start()
         build_own(2 * i, 0)
+        if i == 1:
+            pl.semaphore_wait(go_sem, 1)
+            id_copies[0].start()
     for i in range(4):
         remote(ssend.at[i], srecv.at[i], s_ss, s_rs, partner).start()
     for tile in range(1, 8, 2):
@@ -222,7 +226,7 @@
 
         def take(self, slot, p):
             self.copies[slot, p].wait_recv()
-            block = partner if slot == 3 else mates[0] if slot == 0 and p not in self.direct else peers[slot]
+            block = partner if slot == 3 else peers[slot]
             if p not in self.direct and slot == (1 if p % 2 else 2):
                 self.copies[0, p] = self.copy(block, p, 0, peers[3 - slot])
                 self.copies[0, p].start()
@@ -235,8 +239,7 @@
         def take_forwards(self, n):
             for slot, p, fwd in self.forwards[:n]:
                 fwd.wait_recv()
-                relayed = slot == 0 and p not in self.direct
-                self.ready.append((peers[0] if relayed else mates[slot], p))
+                self.ready.append((mates[slot], p))
             self.forwards = self.forwards[n:]
 
         def own(self, pieces):
@@ -272,7 +275,7 @@
     for flat in range(48):
         u, tile = flat // 8, flat % 8
         while built < 48 and built - flat < 2 or (built < 48 and tile % 2 == 0 and built - flat < lead):
-            if built == 8:
+            if built == 16:
                 take_ids(0)
             if built % 8 == 0:
                 spread_ids(ids_s32, idb, wb, inv, built // 8)
@@ -419,6 +422,7 @@
                 dma, dma((12,)),
                 dma, dma((28,)),
                 dma, dma((28,)),
+                pltpu.SemaphoreType.REGULAR,
             ],
             compiler_params=pltpu.CompilerParams(
                 collective_id=0, has_side_effects=True, vmem_limit_bytes=32 * 1024 * 1024

time: 33.1 us -> 33.7 us (1.018)
  Pallas kernels: 32.3 us -> 33 us
    pallas_call x1, Pallas kernels: 32.3 us -> 33 us  [device_step(): pl.pallas_call(kernel, out_shape=jax.ShapeDtypeStruct((7, BLK), F32), in_...]
where the time goes in v11:
time: 33.7 us; the launch traced here: 33.6 us
  Pallas kernels  33 us (98%)
  local copies, waits for them, and re-layouts  0.61 us (2%)
    pallas_call x1, Pallas kernels, device_step(): pl.pallas_call(kernel, out_shape=jax.ShapeDtypeStruct((7, BLK), F32), in_...  33 us

profile of v11, /device:TPU:0, one launch (start us, length us, event | category | flops | bytes accessed | tf_op | source)
XLA Modules:
  0.0 33.6 jit_solution(13186081200030544211)
XLA Ops:
  0.0 33.0 %graphsage.1 = f32[7,512]{1,0:T(8,128)S(1)} custom-call(bf16[192,4096]{1,0:T(8,128)(2,1)} %bitcast.7, bf16[192,128]{1,0:T(8,128)(2,1)} %ws1_hbm.1, bf16[192,128]{1,0:T(8,128)(2,1)} %wn1_hbm.1, s32[10,512]{1,0:T(8,128)} %bitcast.8, s32[10,512]{1,0:T(8,128)} %bitcast.9, bf16[128,128]{1,0:T(8,128)(2,1)} %ws2_hbm.1, bf16[128,128]{1,0:T(8,128)(2,1)} %wn2_hbm.1, ...), custom_call_target="tpu_custom_call" | custom-call | tf_op jit(solution)/shard_map/graphsage/pallas_call | solution.py:378
  33.0 0.6 %copy.11 = f32[512,7]{0,1:T(8,128)} copy(f32[512,7]{0,1:T(8,128)S(1)} %bitcast.6) | data formatting | bytes 28672

commit v12 on v11

--- a/solution.py
+++ b/solution.py
@@ -18,7 +18,7 @@
 F32 = jnp.float32
 
 
-UNITS = (((2, 0), (1, 0)), ((2, 1), (1, 1)), ((0, 0), (0, 1)), ((0, 2), (0, 3)), ((2, 2), (1, 2)), ((2, 3), (1, 3)))
+UNITS = (((2, 0), (1, 0)), ((0, 0), (0, 1)), ((0, 2), (0, 3)), ((2, 1), (1, 1)), ((2, 2), (1, 2)), ((2, 3), (1, 3)))
 OWN = 6
 RING = 6
 Q = 128
@@ -275,7 +275,7 @@
     for flat in range(48):
         u, tile = flat // 8, flat % 8
         while built < 48 and built - flat < 2 or (built < 48 and tile % 2 == 0 and built - flat < lead):
-            if built == 16:
+            if built == 8:
                 take_ids(0)
             if built % 8 == 0:
                 spread_ids(ids_s32, idb, wb, inv, built // 8)

time: 33.7 us -> 33.3 us (0.988)
  Pallas kernels: 33 us -> 32.6 us
    pallas_call x1, Pallas kernels: 33 us -> 32.6 us  [device_step(): pl.pallas_call(kernel, out_shape=jax.ShapeDtypeStruct((7, BLK), F32), in_...]
where the time goes in v12:
time: 33.3 us; the launch traced here: 33.2 us
  Pallas kernels  32.6 us (98%)
  local copies, waits for them, and re-layouts  0.61 us (2%)
    pallas_call x1, Pallas kernels, device_step(): pl.pallas_call(kernel, out_shape=jax.ShapeDtypeStruct((7, BLK), F32), in_...  32.6 us

profile of v12, /device:TPU:0, one launch (start us, length us, event | category | flops | bytes accessed | tf_op | source)
XLA Modules:
  0.0 33.2 jit_solution(16402229505790040693)
XLA Ops:
  0.0 32.6 %graphsage.1 = f32[7,512]{1,0:T(8,128)S(1)} custom-call(bf16[192,4096]{1,0:T(8,128)(2,1)} %bitcast.7, bf16[192,128]{1,0:T(8,128)(2,1)} %ws1_hbm.1, bf16[192,128]{1,0:T(8,128)(2,1)} %wn1_hbm.1, s32[10,512]{1,0:T(8,128)} %bitcast.8, s32[10,512]{1,0:T(8,128)} %bitcast.9, bf16[128,128]{1,0:T(8,128)(2,1)} %ws2_hbm.1, bf16[128,128]{1,0:T(8,128)(2,1)} %wn2_hbm.1, ...), custom_call_target="tpu_custom_call" | custom-call | tf_op jit(solution)/shard_map/graphsage/pallas_call | solution.py:378
  32.6 0.6 %copy.11 = f32[512,7]{0,1:T(8,128)} copy(f32[512,7]{0,1:T(8,128)S(1)} %bitcast.6) | data formatting | bytes 28672

commit v13 on v10

--- a/solution.py
+++ b/solution.py
@@ -149,6 +149,8 @@
         remote(ssend.at[i], srecv.at[i], s_ss, s_rs, partner).start()
     for tile in range(1, 8, 2):
         build_own(tile, 0)
+    for tile in range(8):
+        build_own(tile, 1)
     for cp in late_cps:
         cp.wait()
     w2st[...] = ws2[...].T
@@ -281,20 +283,18 @@
         part = dot_from(flat)
         low = part[0] if low is None else low + part[0]
         high = part[1] if high is None else high + part[1]
-        if u == 1:
-            own = own_piece(tile, 0) if own is None else own + own_piece(tile, 0)
+        if u in (1, 3):
+            own = own_piece(tile, u // 2) if own is None else own + own_piece(tile, u // 2)
         if tile == 7:
             if u == 0:
                 drain(srecv, s_rs)
             finish_unit(u, low, high)
             low = high = None
-            if u == 1:
-                own_base(0, own)
-    for tile in range(8):
-        build_own(tile, 1)
+            if u in (1, 3):
+                own_base(u // 2, own)
+                own = None
     finish_quarter(0)
     finish_quarter(1)
-    own_base(1, sum(own_piece(b, 1) for b in range(N_DEV)))
     finish_quarter(2)
     finish_quarter(3)
     g1.own(4)

time: 33.1 us -> 33 us (level)
  no operation moved by 1% of the time
where the time goes in v13:
time: 33 us; the launch traced here: 32.9 us
  Pallas kernels  32.3 us (98%)
  local copies, waits for them, and re-layouts  0.61 us (2%)
    pallas_call x1, Pallas kernels, device_step(): pl.pallas_call(kernel, out_shape=jax.ShapeDtypeStruct((7, BLK), F32), in_...  32.3 us

profile of v13, /device:TPU:0, one launch (start us, length us, event | category | flops | bytes accessed | tf_op | source)
XLA Modules:
  0.0 32.9 jit_solution(17851153803596839932)
XLA Ops:
  0.0 32.3 %graphsage.1 = f32[7,512]{1,0:T(8,128)S(1)} custom-call(bf16[192,4096]{1,0:T(8,128)(2,1)} %bitcast.7, bf16[192,128]{1,0:T(8,128)(2,1)} %ws1_hbm.1, bf16[192,128]{1,0:T(8,128)(2,1)} %wn1_hbm.1, s32[10,512]{1,0:T(8,128)} %bitcast.8, s32[10,512]{1,0:T(8,128)} %bitcast.9, bf16[128,128]{1,0:T(8,128)(2,1)} %ws2_hbm.1, bf16[128,128]{1,0:T(8,128)(2,1)} %wn2_hbm.1, ...), custom_call_target="tpu_custom_call" | custom-call | tf_op jit(solution)/shard_map/graphsage/pallas_call | solution.py:375
  32.3 0.6 %copy.11 = f32[512,7]{0,1:T(8,128)} copy(f32[512,7]{0,1:T(8,128)S(1)} %bitcast.6) | data formatting | bytes 28672

commit v14 on v13

--- a/solution.py
+++ b/solution.py
@@ -306,11 +306,11 @@
     for p in range(4):
         g1.take(3, p)
     g1.add()
-    g1.take(0, 0)
-    g1.take(0, 1)
+    for slot, p in ((2, 3), (1, 3), (0, 0), (0, 1)):
+        g1.take(slot, p)
     g1.take_forwards(6)
     g1.add()
-    for slot, p in ((2, 3), (1, 3), (0, 3), (0, 2)):
+    for slot, p in ((0, 3), (0, 2)):
         g1.take(slot, p)
     g1.add()
     g1.take_forwards(4)

time: 33 us -> 33 us (level)
  no operation moved by 1% of the time
where the time goes in v14:
time: 33 us; the launch traced here: 32.9 us
  Pallas kernels  32.3 us (98%)
  local copies, waits for them, and re-layouts  0.61 us (2%)
    pallas_call x1, Pallas kernels, device_step(): pl.pallas_call(kernel, out_shape=jax.ShapeDtypeStruct((7, BLK), F32), in_...  32.3 us

profile of v14, /device:TPU:0, one launch (start us, length us, event | category | flops | bytes accessed | tf_op | source)
XLA Modules:
  0.0 32.9 jit_solution(18369681669968697041)
XLA Ops:
  0.0 32.3 %graphsage.1 = f32[7,512]{1,0:T(8,128)S(1)} custom-call(bf16[192,4096]{1,0:T(8,128)(2,1)} %bitcast.7, bf16[192,128]{1,0:T(8,128)(2,1)} %ws1_hbm.1, bf16[192,128]{1,0:T(8,128)(2,1)} %wn1_hbm.1, s32[10,512]{1,0:T(8,128)} %bitcast.8, s32[10,512]{1,0:T(8,128)} %bitcast.9, bf16[128,128]{1,0:T(8,128)(2,1)} %ws2_hbm.1, bf16[128,128]{1,0:T(8,128)(2,1)} %wn2_hbm.1, ...), custom_call_target="tpu_custom_call" | custom-call | tf_op jit(solution)/shard_map/graphsage/pallas_call | solution.py:375
  32.3 0.6 %copy.11 = f32[512,7]{0,1:T(8,128)} copy(f32[512,7]{0,1:T(8,128)S(1)} %bitcast.6) | data formatting | bytes 28672

commit v15 on v14

--- a/solution.py
+++ b/solution.py
@@ -248,7 +248,7 @@
             acc[...] += sum(own_dot(self.h, b, p) for b, p in self.ready)
             self.ready = []
 
-    g1 = Gather(h1, g1_ss, g1_rs, direct=(3,))
+    g1 = Gather(h1, g1_ss, g1_rs, direct=(2, 3))
     g2 = Gather(h2, g2_ss, g2_rs, direct=())
 
     def finish_quarter(q):

time: 33 us -> 33.4 us (1.012)
    pallas_call x1, Pallas kernels: 32.3 us -> 32.6 us  [device_step(): pl.pallas_call(kernel, out_shape=jax.ShapeDtypeStruct((7, BLK), F32), in_...]
where the time goes in v15:
time: 33.4 us; the launch traced here: 33.3 us
  Pallas kernels  32.6 us (98%)
  local copies, waits for them, and re-layouts  0.61 us (2%)
    pallas_call x1, Pallas kernels, device_step(): pl.pallas_call(kernel, out_shape=jax.ShapeDtypeStruct((7, BLK), F32), in_...  32.6 us

profile of v15, /device:TPU:0, one launch (start us, length us, event | category | flops | bytes accessed | tf_op | source)
XLA Modules:
  0.0 33.3 jit_solution(14066460930059451819)
XLA Ops:
  0.0 32.6 %graphsage.1 = f32[7,512]{1,0:T(8,128)S(1)} custom-call(bf16[192,4096]{1,0:T(8,128)(2,1)} %bitcast.7, bf16[192,128]{1,0:T(8,128)(2,1)} %ws1_hbm.1, bf16[192,128]{1,0:T(8,128)(2,1)} %wn1_hbm.1, s32[10,512]{1,0:T(8,128)} %bitcast.8, s32[10,512]{1,0:T(8,128)} %bitcast.9, bf16[128,128]{1,0:T(8,128)(2,1)} %ws2_hbm.1, bf16[128,128]{1,0:T(8,128)(2,1)} %wn2_hbm.1, ...), custom_call_target="tpu_custom_call" | custom-call | tf_op jit(solution)/shard_map/graphsage/pallas_call | solution.py:375
  32.6 0.6 %copy.11 = f32[512,7]{0,1:T(8,128)} copy(f32[512,7]{0,1:T(8,128)S(1)} %bitcast.6) | data formatting | bytes 28672

commit v16 on v15

--- a/solution.py
+++ b/solution.py
@@ -248,7 +248,7 @@
             acc[...] += sum(own_dot(self.h, b, p) for b, p in self.ready)
             self.ready = []
 
-    g1 = Gather(h1, g1_ss, g1_rs, direct=(2, 3))
+    g1 = Gather(h1, g1_ss, g1_rs, direct=())
     g2 = Gather(h2, g2_ss, g2_rs, direct=())
 
     def finish_quarter(q):
@@ -310,7 +310,7 @@
         g1.take(slot, p)
     g1.take_forwards(6)
     g1.add()
-    for slot, p in ((0, 3), (0, 2)):
+    for slot, p in ((0, 2), (0, 3)):
         g1.take(slot, p)
     g1.add()
     g1.take_forwards(4)

time: 33.4 us -> 33.7 us (level)
  Pallas kernels: 32.6 us -> 33 us
    pallas_call x1, Pallas kernels: 32.6 us -> 33 us  [device_step(): pl.pallas_call(kernel, out_shape=jax.ShapeDtypeStruct((7, BLK), F32), in_...]
where the time goes in v16:
time: 33.7 us; the launch traced here: 33.6 us
  Pallas kernels  33 us (98%)
  local copies, waits for them, and re-layouts  0.61 us (2%)
    pallas_call x1, Pallas kernels, device_step(): pl.pallas_call(kernel, out_shape=jax.ShapeDtypeStruct((7, BLK), F32), in_...  33 us

profile of v16, /device:TPU:0, one launch (start us, length us, event | category | flops | bytes accessed | tf_op | source)
XLA Modules:
  0.0 33.6 jit_solution(932476541526458731)
XLA Ops:
  0.0 33.0 %graphsage.1 = f32[7,512]{1,0:T(8,128)S(1)} custom-call(bf16[192,4096]{1,0:T(8,128)(2,1)} %bitcast.7, bf16[192,128]{1,0:T(8,128)(2,1)} %ws1_hbm.1, bf16[192,128]{1,0:T(8,128)(2,1)} %wn1_hbm.1, s32[10,512]{1,0:T(8,128)} %bitcast.8, s32[10,512]{1,0:T(8,128)} %bitcast.9, bf16[128,128]{1,0:T(8,128)(2,1)} %ws2_hbm.1, bf16[128,128]{1,0:T(8,128)(2,1)} %wn2_hbm.1, ...), custom_call_target="tpu_custom_call" | custom-call | tf_op jit(solution)/shard_map/graphsage/pallas_call | solution.py:375
  33.0 0.6 %copy.11 = f32[512,7]{0,1:T(8,128)} copy(f32[512,7]{0,1:T(8,128)S(1)} %bitcast.6) | data formatting | bytes 28672

commit v17 on v13

--- a/solution.py
+++ b/solution.py
@@ -294,8 +294,8 @@
                 own_base(u // 2, own)
                 own = None
     finish_quarter(0)
+    finish_quarter(2)
     finish_quarter(1)
-    finish_quarter(2)
     finish_quarter(3)
     g1.own(4)
     for g in range(2):

time: 33 us -> 34 us (1.030)
  Pallas kernels: 32.3 us -> 33.3 us
    pallas_call x1, Pallas kernels: 32.3 us -> 33.3 us  [device_step(): pl.pallas_call(kernel, out_shape=jax.ShapeDtypeStruct((7, BLK), F32), in_...]
where the time goes in v17:
time: 34 us; the launch traced here: 33.9 us
  Pallas kernels  33.3 us (98%)
  local copies, waits for them, and re-layouts  0.61 us (2%)
    pallas_call x1, Pallas kernels, device_step(): pl.pallas_call(kernel, out_shape=jax.ShapeDtypeStruct((7, BLK), F32), in_...  33.3 us

profile of v17, /device:TPU:0, one launch (start us, length us, event | category | flops | bytes accessed | tf_op | source)
XLA Modules:
  0.0 33.9 jit_solution(4043242147174102310)
XLA Ops:
  0.0 33.3 %graphsage.1 = f32[7,512]{1,0:T(8,128)S(1)} custom-call(bf16[192,4096]{1,0:T(8,128)(2,1)} %bitcast.7, bf16[192,128]{1,0:T(8,128)(2,1)} %ws1_hbm.1, bf16[192,128]{1,0:T(8,128)(2,1)} %wn1_hbm.1, s32[10,512]{1,0:T(8,128)} %bitcast.8, s32[10,512]{1,0:T(8,128)} %bitcast.9, bf16[128,128]{1,0:T(8,128)(2,1)} %ws2_hbm.1, bf16[128,128]{1,0:T(8,128)(2,1)} %wn2_hbm.1, ...), custom_call_target="tpu_custom_call" | custom-call | tf_op jit(solution)/shard_map/graphsage/pallas_call | solution.py:375
  33.3 0.6 %copy.11 = f32[512,7]{0,1:T(8,128)} copy(f32[512,7]{0,1:T(8,128)S(1)} %bitcast.6) | data formatting | bytes 28672
